TPU v7x, 64 devices: a 2x2x8 block of a 4x4x8 slice. The times are simulated.
64 devices in a mesh: dp: 4 (over x, y), ep: 16 (over z, core).
Axes of the slice: x: 2, y: 2, z: 8, core: 2. Of those that a mesh axis runs over, the one named last changes fastest.
The devices are a block of a 4x4x8 slice.
Arguments:
- tokens: bfloat16 [32768, 2048], P(('dp', 'ep')), parts along dimension 0
- w_router: bfloat16 [2048, 64], replicated
- expert_ids: int32 [32768, 6], P(('dp', 'ep')), parts along dimension 0
- w_gate: bfloat16 [64, 2048, 1408], P('ep')
- w_up: bfloat16 [64, 2048, 1408], P('ep')
- w_down: bfloat16 [64, 1408, 2048], P('ep')
- shared_gate: bfloat16 [2048, 2816], replicated
- shared_up: bfloat16 [2048, 2816], replicated
- shared_down: bfloat16 [2816, 2048], replicated
Outputs:
- output: bfloat16 [32768, 2048], P(('dp', 'ep')), parts along dimension 0
There are 4 independent parts. A program takes and returns all parts, laid end to end along the dimension named above; an argument that names none is the same for every part.
All inputs are finite; a program needn't handle non-finite values.
Results may differ from a plain program's by a relative error of at most 0.00812751.
Values are sent between devices in bfloat16 or wider.
A program may use at most 768 MiB of HBM per device.

v0:
```python
import functools

import jax
import jax.numpy as jnp
from jax import lax
from jax.experimental import pallas as pl
from jax.experimental.pallas import tpu as pltpu
from jax.sharding import PartitionSpec as P


MESH = pl.DeviceIdType.MESH
VMEM_LIMIT = 60 * 1024 * 1024


def capacity_of(tok_dev, top_k, num_exp):
    base_load = tok_dev * top_k // num_exp
    return base_load + base_load // 2 + min(tok_dev * top_k % num_exp, 1)


def gate_values(tok_rows, w_router, ids_loc):
    logits = jnp.dot(tok_rows, w_router, preferred_element_type=jnp.float32)
    expert_range = jnp.arange(w_router.shape[1], dtype=jnp.int32)
    hit = ids_loc[:, :, None] == expert_range[None, None, :]
    picked = jnp.sum(jnp.where(hit, logits[:, None, :], 0.0), axis=2)
    return jax.nn.softmax(picked, axis=-1)


def exchange_kernel(group, mine_ref, all_ref, send_sem, recv_sem):
    me = lax.axis_index('ep')
    barrier = pltpu.get_barrier_semaphore()
    for i in range(1, group):
        pl.semaphore_signal(barrier, inc=1, device_id={'ep': lax.rem(me + i, group)}, device_id_type=MESH)
    pl.semaphore_wait(barrier, group - 1)
    copies = []
    for i in range(1, group):
        copies.append(pltpu.make_async_remote_copy(
            src_ref=mine_ref,
            dst_ref=all_ref.at[me],
            send_sem=send_sem.at[i],
            recv_sem=recv_sem.at[i],
            device_id={'ep': lax.rem(me + i, group)},
            device_id_type=MESH,
        ))
    for copy in copies:
        copy.start()
    all_ref[pl.ds(me, 1)] = mine_ref[...][None]
    for copy in copies:
        copy.wait()


def exchange(mine, group):
    return pl.pallas_call(
        functools.partial(exchange_kernel, group),
        out_shape=jax.ShapeDtypeStruct((group,) + mine.shape, mine.dtype),
        in_specs=[pl.BlockSpec(memory_space=pltpu.VMEM)],
        out_specs=pl.BlockSpec(memory_space=pltpu.VMEM),
        scratch_shapes=[pltpu.SemaphoreType.DMA((group,)), pltpu.SemaphoreType.DMA((group,))],
        compiler_params=pltpu.CompilerParams(collective_id=0, has_side_effects=True),
    )(mine)


def dispatch_kernel(count, slots, *refs):
    chunks, rank_ref = refs[:count], refs[count]
    out_ref, buf, sem = refs[-3:]
    i = pl.program_id(0)
    num_loc, tok_dev = rank_ref.shape[1], rank_ref.shape[2]

    def fetch(k):
        return pltpu.make_async_copy(chunks[k], buf.at[k % 2], sem.at[k % 2])

    for k in range(count):
        @pl.when(i == k)
        def _(k=k):
            if k == 0:
                fetch(0).start()
            if k + 1 < count:
                fetch(k + 1).start()
            fetch(k).wait()
    slot_range = lax.broadcasted_iota(jnp.int32, (num_loc, slots, tok_dev), 1).astype(jnp.float32)
    chosen = rank_ref[0][:, None, :] == slot_range
    one_hot = jnp.where(chosen, 1.0, 0.0).reshape(num_loc * slots, tok_dev).astype(jnp.bfloat16)
    rows = jnp.dot(one_hot, buf[i % 2], preferred_element_type=jnp.float32)
    out_ref[...] = rows.astype(jnp.bfloat16).reshape(out_ref.shape)


def dispatch_rows(chunks, ranks, slots, first, total, so_far=None):
    count = len(chunks)
    tok_dev, width = chunks[0].shape
    num_loc = ranks.shape[1]
    flops = 2 * count * num_loc * slots * tok_dev * width
    kept = [] if so_far is None else [so_far]
    return pl.pallas_call(
        functools.partial(dispatch_kernel, count, slots),
        grid=(count,),
        out_shape=jax.ShapeDtypeStruct((num_loc, total * slots, width), jnp.bfloat16),
        in_specs=[pl.BlockSpec(memory_space=pl.ANY)] * count + [pl.BlockSpec((1, num_loc, tok_dev), lambda i: (i, 0, 0))] + [pl.BlockSpec(memory_space=pl.ANY)] * len(kept),
        out_specs=pl.BlockSpec((num_loc, slots, width), lambda i: (0, i + first, 0)),
        input_output_aliases={count + 1: 0} if kept else {},
        scratch_shapes=[pltpu.VMEM((2, tok_dev, width), jnp.bfloat16), pltpu.SemaphoreType.DMA((2,))],
        cost_estimate=pl.CostEstimate(flops=flops, bytes_accessed=4 * count * tok_dev * width, transcendentals=0),
        compiler_params=pltpu.CompilerParams(vmem_limit_bytes=VMEM_LIMIT),
    )(*chunks, ranks, *kept)


def expert_kernel(*refs):
    rows_ref, gate_ref, up_ref, down_ref = refs[:4]
    out_ref = refs[-1]
    rows = rows_ref[0]
    gate_act = jnp.dot(rows, gate_ref[0], preferred_element_type=jnp.float32)
    up_act = jnp.dot(rows, up_ref[0], preferred_element_type=jnp.float32)
    hidden = (jax.nn.silu(gate_act) * up_act).astype(jnp.bfloat16)
    out_ref[0] = jnp.dot(hidden, down_ref[0], preferred_element_type=jnp.float32).astype(jnp.bfloat16)


def expert_mlp(rows, w_gate, w_up, w_down, first, count, so_far=None):
    rows_per, width = rows.shape[1:]
    inner = w_gate.shape[2]
    kept = [] if so_far is None else [so_far]
    return pl.pallas_call(
        expert_kernel,
        grid=(count,),
        out_shape=jax.ShapeDtypeStruct(rows.shape, jnp.bfloat16),
        in_specs=[
            pl.BlockSpec((1, rows_per, width), lambda e: (e + first, 0, 0)),
            pl.BlockSpec((1, width, inner), lambda e: (e + first, 0, 0)),
            pl.BlockSpec((1, width, inner), lambda e: (e + first, 0, 0)),
            pl.BlockSpec((1, inner, width), lambda e: (e + first, 0, 0)),
        ] + [pl.BlockSpec(memory_space=pl.ANY)] * len(kept),
        out_specs=pl.BlockSpec((1, rows_per, width), lambda e: (e + first, 0, 0)),
        input_output_aliases={4: 0} if kept else {},
        cost_estimate=pl.CostEstimate(flops=6 * count * rows_per * width * inner, bytes_accessed=6 * count * width * inner, transcendentals=count * rows_per * inner),
        compiler_params=pltpu.CompilerParams(vmem_limit_bytes=VMEM_LIMIT),
    )(rows, w_gate, w_up, w_down, *kept)


def combine_kernel(sets, adds, *refs):
    row_refs, refs = refs[:sets], refs[sets:]
    rank_refs, refs = refs[:sets], refs[sets:]
    gate_refs, refs = refs[:sets], refs[sets:]
    add_refs, (out_ref, weights) = refs[:adds], refs[adds:]
    num_loc, slots = row_refs[0].shape[0], row_refs[0].shape[1]
    tok_dev = out_ref.shape[0]

    @pl.when(pl.program_id(0) == 0)
    def _():
        slot_range = lax.broadcasted_iota(jnp.int32, (num_loc, slots, tok_dev), 1).astype(jnp.float32)
        for s in range(sets):
            chosen = rank_refs[s][0][:, None, :] == slot_range
            gate = gate_refs[s][0]
            high = gate.astype(jnp.bfloat16).astype(jnp.float32)
            rest = gate - high
            middle = rest.astype(jnp.bfloat16).astype(jnp.float32)
            low = rest - middle
            for k, term in enumerate((high, middle, low)):
                value = jnp.where(chosen, term[:, None, :], 0.0).reshape(num_loc * slots, tok_dev)
                at = (3 * s + k) * num_loc * slots
                weights[at:at + num_loc * slots, :] = value.astype(jnp.bfloat16)

    total = None
    for add_ref in add_refs:
        value = add_ref[...].astype(jnp.float32)
        total = value if total is None else total + value
    rows = []
    for s in range(sets):
        rows += [row_refs[s][...].reshape(num_loc * slots, out_ref.shape[1])] * 3
    rows = jnp.concatenate(rows, axis=0)
    value = lax.dot_general(weights[...], rows, (((0,), (0,)), ((), ())), preferred_element_type=jnp.float32)
    total = value if total is None else total + value
    out_ref[...] = total.astype(out_ref.dtype)


def combine_rows(pieces, ranks, gates, slots, added, out_dtype=jnp.float32):
    num_loc, tok_dev = ranks.shape[1], ranks.shape[2]
    width = pieces[0][0].shape[2]
    cols = width // 2
    row_specs = [pl.BlockSpec((num_loc, slots, cols), lambda j, b=b: (0, b, j)) for _, b, _ in pieces]
    table_specs = [pl.BlockSpec((1, num_loc, tok_dev), lambda j, t=t: (t, 0, 0)) for _, _, t in pieces]
    flat_spec = pl.BlockSpec((tok_dev, cols), lambda j: (0, j))
    flops = 6 * len(pieces) * num_loc * slots * tok_dev * width
    return pl.pallas_call(
        functools.partial(combine_kernel, len(pieces), len(added)),
        grid=(2,),
        out_shape=jax.ShapeDtypeStruct((tok_dev, width), out_dtype),
        in_specs=row_specs + table_specs + table_specs + [flat_spec] * len(added),
        out_specs=flat_spec,
        scratch_shapes=[pltpu.VMEM((len(pieces) * 3 * num_loc * slots, tok_dev), jnp.bfloat16)],
        cost_estimate=pl.CostEstimate(flops=flops, bytes_accessed=4 * tok_dev * width * (1 + len(added)), transcendentals=0),
        compiler_params=pltpu.CompilerParams(vmem_limit_bytes=VMEM_LIMIT),
    )(*[p[0] for p in pieces], *[ranks] * len(pieces), *[gates] * len(pieces), *added)


def solution(mesh):
    group = mesh.shape['ep']
    ring = group // 2
    far = ring // 2
    row_spec = P(('dp', 'ep'), None)
    full_spec = P(None, None)
    expert_spec = P('ep', None, None)

    def index_of(z, core):
        return (z % ring) * 2 + core

    away_perm = [(index_of(z, c), index_of(z + (1 - 2 * c), c)) for z in range(ring) for c in range(2)]
    back_perm = [(dst, src) for src, dst in away_perm]
    swap_perm = [(i, i ^ 1) for i in range(group)]
    away_cross = [(src, dst ^ 1) for src, dst in away_perm]
    back_cross = [(src, dst ^ 1) for src, dst in back_perm]

    perms = {'away': away_perm, 'back': back_perm, 'swap': swap_perm, 'away_cross': away_cross, 'back_cross': back_cross}

    def send(way, value):
        return lax.ppermute(value, 'ep', perms[way])

    def device_step(tok_rows, w_router, ids_loc, w_gate, w_up, w_down, shared_gate, shared_up, shared_down):
        tok_dev, top_k = ids_loc.shape
        num_exp = w_router.shape[1]
        num_loc = w_gate.shape[0]
        capacity = capacity_of(tok_dev, top_k, num_exp)
        slots = -(-capacity // 16) * 16
        me = lax.axis_index('ep')
        core = me % 2
        z = me // 2
        sign = 1 - 2 * core
        last = [ids_loc]

        def step(fn, *args):
            args, _ = lax.optimization_barrier((args, last[0]))
            out = fn(*args)
            last[0] = out
            return out

        def after(value, other):
            return lax.optimization_barrier((value, other))[0]

        def src(d, other):
            if other:
                return index_of(z + sign * d, 1 - core)
            return index_of(z - sign * d, core)

        def meta_of(rows, w_r, ids):
            gates = gate_values(rows, w_r, ids)
            return jnp.concatenate([ids.astype(jnp.float32).T, gates.T], axis=0).reshape(-1, 128)

        def gate_act_of(rows, w_one):
            return jnp.dot(rows, w_one, preferred_element_type=jnp.float32)

        def hidden_of(rows, gate_act, w_three):
            up_act = jnp.dot(rows, w_three, preferred_element_type=jnp.float32)
            return (jax.nn.silu(gate_act) * up_act).astype(jnp.bfloat16)

        def down_of(hidden, w_two):
            return jnp.dot(hidden, w_two, preferred_element_type=jnp.float32).astype(jnp.bfloat16)

        pairs = {}
        sources, holders = [], []

        def need(name, source, holder):
            pairs[name] = len(sources)
            sources.append(source)
            holders.append(holder)

        for d in range(far + 1):
            need(('a', d, False), src(d, False), me)
            need(('a', d, True), src(d, True), me)
            need(('sa', d), src(d, False), index_of(z, 1 - core))
        for d in range(1, far):
            need(('b', d, False), src(-d, False), me)
            need(('b', d, True), src(-d, True), me)
            need(('sb', d), src(-d, False), index_of(z, 1 - core))
        for other in (False, True):
            held = core if not other else 1 - core
            need(('ra', other), src(far - 1, False), index_of(z + sign, held))
            need(('rb', other), src(-(far - 2), False), index_of(z - sign, held))

        def tables_of(m):
            picked = jnp.take(m.reshape(group, 2 * top_k, tok_dev), jnp.stack(sources), axis=0)
            ids = picked[:, None, :top_k, :].astype(jnp.int32)
            gates = picked[:, None, top_k:2 * top_k, :]
            experts = jnp.stack(holders)[:, None] * num_loc + jnp.arange(num_loc, dtype=jnp.int32)[None, :]
            hit = ids == experts[:, :, None, None]
            named = jnp.any(hit, axis=2)
            gate_of = jnp.sum(jnp.where(hit, gates, 0.0), axis=2)
            tok_range = jnp.arange(tok_dev)
            before = (tok_range[:, None] < tok_range[None, :]).astype(jnp.bfloat16)
            rank = jnp.einsum('net,tu->neu', named.astype(jnp.bfloat16), before, preferred_element_type=jnp.float32)
            return jnp.where(named, rank, -1.0), gate_of

        a_own, b_own = [tok_rows, send('away', tok_rows)], [None, send('back', tok_rows)]
        meta = step(meta_of, tok_rows, w_router, ids_loc)
        gate_act = step(gate_act_of, tok_rows, shared_gate)
        hidden = step(hidden_of, tok_rows, gate_act, shared_up)
        shared_out = step(down_of, hidden, shared_down)
        a_own.append(send('away', a_own[1]))
        meta = step(lambda m: exchange(m, group), meta)
        a_own.append(send('away', a_own[2]))
        ranks, gates = step(tables_of, meta)
        half = num_loc // 2

        def mlp_first(rows):
            return step(lambda r, *w: expert_mlp(r, *w, 0, half), rows, w_gate, w_up, w_down)

        def mlp_rest(rows, so_far):
            return step(lambda r, s, *w: expert_mlp(r, *w, half, num_loc - half, s), rows, so_far, w_gate, w_up, w_down)

        def chunk_of(name):
            kind, d, other = name
            return {'a': (a_own, a_oth), 'b': (b_own, b_oth)}[kind][other][d]

        def gather_rows(names, start, stop, so_far=None):
            order = jnp.array([pairs[n] for n in names[start:stop]])
            chunks = [chunk_of(n) for n in names[start:stop]]
            return step(lambda c, r, s: dispatch_rows(c, r[order], slots, start, len(names), s), chunks, ranks, so_far)

        def blocks(out, start, stop):
            return step(lambda o: o[:, start * slots:stop * slots], out)

        def total(pieces, added=(), out_dtype=jnp.float32):
            def run(arrays, r, g, a):
                pieces_in = [(x, b, pairs[n]) for x, (_, b, n) in zip(arrays, pieces)]
                return combine_rows(pieces_in, r, g, slots, a, out_dtype)

            return step(run, [p[0] for p in pieces], ranks, gates, list(added))

        names_0 = [('a', 2, False), ('a', 2, True)]
        names_1 = [('a', far, False), ('a', far, True), ('a', 3, False), ('a', 3, True)]
        names_2 = [('a', 1, False), ('a', 0, False), ('a', 1, True), ('a', 0, True)]
        names_3 = [('b', 3, False), ('b', 3, True), ('b', 2, False), ('b', 1, False), ('b', 2, True), ('b', 1, True)]

        a_oth = [send('swap', tok_rows)] + [send('swap', a_own[d]) for d in range(1, far)]
        b_oth = [None, send('swap', b_own[1])]
        rows_0 = gather_rows(names_0, 0, 2)
        out_0 = mlp_first(rows_0)
        a_own.append(send('away', a_own[3]))
        a_oth.append(send('swap', a_own[far]))
        out_0 = mlp_rest(rows_0, out_0)
        oth_0 = send('swap', blocks(out_0, 1, 2))
        rows_1 = gather_rows(names_1, 2, 4)
        b_own.append(send('back', after(b_own[1], a_own[far])))

        rows_1 = gather_rows(names_1, 0, 2, rows_1)
        out_1 = mlp_first(rows_1)
        b_own.append(send('back', b_own[2]))
        b_oth.append(send('swap', b_own[2]))
        out_1 = mlp_rest(rows_1, out_1)
        got_own = send('back', blocks(out_1, 0, 1))
        got_oth = send('away_cross', blocks(out_1, 1, 2))
        oth_1 = send('swap', blocks(out_1, 3, 4))
        b_oth.append(send('swap', b_own[3]))

        rows_3 = gather_rows(names_3, 0, 6)
        acc_a = send('back', total([(got_own, 0, ('ra', False)), (got_oth, 0, ('ra', True)), (out_1, 2, ('a', 3, False)), (oth_1, 0, ('sa', 3))]))
        out_3 = mlp_first(rows_3)
        out_3 = mlp_rest(rows_3, out_3)
        got_own = send('away', blocks(out_3, 0, 1))
        got_oth = send('back_cross', blocks(out_3, 1, 2))
        oth_3 = send('swap', blocks(out_3, 4, 6))
        acc_a = send('back', total([(out_0, 0, ('a', 2, False)), (oth_0, 0, ('sa', 2))], [acc_a]))
        rows_2 = gather_rows(names_2, 0, 4)
        out_2 = mlp_first(rows_2)
        acc_b = send('away', total([(got_own, 0, ('rb', False)), (got_oth, 0, ('rb', True)), (out_3, 2, ('b', 2, False)), (oth_3, 0, ('sb', 2))]))
        out_2 = mlp_rest(rows_2, out_2)
        oth_2 = send('swap', blocks(out_2, 2, 4))
        here = total([(out_2, 1, ('a', 0, False)), (oth_2, 1, ('sa', 0))], [shared_out])
        acc_a = send('back', total([(out_2, 0, ('a', 1, False)), (oth_2, 0, ('sa', 1))], [acc_a]))
        acc_b = send('away', total([(out_3, 3, ('b', 1, False)), (oth_3, 1, ('sb', 1))], [acc_b]))
        return step(lambda x, a, b: (x + a + b).astype(jnp.bfloat16), here, acc_a, acc_b)


    return jax.shard_map(device_step, mesh=mesh, in_specs=(row_spec, full_spec, row_spec, expert_spec, expert_spec, expert_spec, full_spec, full_spec, full_spec), out_specs=row_spec, check_vma=False)
```

profile of v0, /device:TPU:21, one launch (start us, length us, event | category | flops | bytes accessed | tf_op | source)
XLA Modules:
  0.0 624.1 jit_solution(9220472248763055334)
XLA Ops:
  0.0 7.8 %collective-permute-start = (bf16[512,2048]{1,0:T(8,128)(2,1)}, bf16[512,2048]{1,0:T(8,128)(2,1)}, u32[]{:S(2)}, u32[]{:S(2)}) collective-permute-start(bf16[512,2048]{1,0:T(8,128)(2,1)} %refs_1_.6), channel_id=1, source_target_pairs={{0,2},{1,15},{2,4},{3,1},{4,6},{5,3},{6,8},{7,5},{8,10},{9,7},{10,... | collective-permute-start | bytes 6291464 | tf_op jit(solution)/shard_map/ppermute | solution.py:212
  7.8 23.3 %collective-permute-done.refs_0_ = bf16[512,2048]{1,0:T(8,128)(2,1)} collective-permute-done((bf16[512,2048]{1,0:T(8,128)(2,1)}, bf16[512,2048]{1,0:T(8,128)(2,1)}, u32[]{:S(2)}, u32[]{:S(2)}) %collective-permute-start) | collective-permute-done | bytes 2097184 | tf_op jit(solution)/shard_map/ppermute | solution.py:212
  31.1 3.1 collective-permute-start.3
  34.2 2.4 fusion.8
  37.5 40.3 %collective-permute-done.3.refs_0_ = bf16[512,2048]{1,0:T(8,128)(2,1)} collective-permute-done((bf16[512,2048]{1,0:T(8,128)(2,1)}, bf16[512,2048]{1,0:T(8,128)(2,1)}, u32[]{:S(2)}, u32[]{:S(2)}) %collective-permute-start.3) | collective-permute-done | bytes 2097184 | tf_op jit(solution)/shard_map/ppermute | solution.py:212
  77.7 3.4 collective-permute-start.6
  82.5 11.2 %fusion.9 = f32[512,2816]{1,0:T(8,128)} fusion(bf16[512,2048]{1,0:T(8,128)(2,1)S(1)} %copy-done.4, bf16[2048,2816]{1,0:T(8,128)(2,1)} %param.20), kind=kOutput, calls=%fused_computation.40 | convolution fusion | flops 5905580032 | bytes 19398656 | tf_op jit(solution)/shard_map/dot_general | solution.py:245
  93.8 10.7 %collective-permute-done.6.refs_0_ = bf16[512,2048]{1,0:T(8,128)(2,1)} collective-permute-done((bf16[512,2048]{1,0:T(8,128)(2,1)}, bf16[512,2048]{1,0:T(8,128)(2,1)}, u32[]{:S(2)}, u32[]{:S(2)}) %collective-permute-start.6) | collective-permute-done | bytes 2097184 | tf_op jit(solution)/shard_map/ppermute | solution.py:212
  104.4 3.1 collective-permute-start.7
  107.6 9.7 %multiply_convert_fusion = bf16[512,2816]{1,0:T(8,128)(2,1)} fusion(f32[512,2816]{1,0:T(8,128)} %fusion.9, bf16[512,2048]{1,0:T(8,128)(2,1)S(1)} %copy-done.4, bf16[2048,2816]{1,0:T(8,128)(2,1)S(1)} %copy-done.10), kind=kOutput, calls=%fused_computation.6 | convolution fusion | flops 5914230784 | bytes 22282240 | tf_op jit(solution)/shard_map/dot_general | solution.py:248
  117.3 13.5 %collective-permute-done.7.refs_0_ = bf16[512,2048]{1,0:T(8,128)(2,1)} collective-permute-done((bf16[512,2048]{1,0:T(8,128)(2,1)}, bf16[512,2048]{1,0:T(8,128)(2,1)}, u32[]{:S(2)}, u32[]{:S(2)}) %collective-permute-start.7) | collective-permute-done | bytes 2097184 | tf_op jit(solution)/shard_map/ppermute | solution.py:212
  130.9 8.8 %convolution_convert_fusion.refs_6_ = bf16[512,2048]{1,0:T(8,128)(2,1)} fusion(bf16[512,2816]{1,0:T(8,128)(2,1)} %multiply_convert_fusion, bf16[2816,2048]{1,0:T(8,128)(2,1)S(1)} %bitcast.53), kind=kOutput, calls=%fused_computation.8 | convolution fusion | flops 5906628608 | bytes 16515072 | tf_op jit(solution)/shard_map/dot_general | solution.py:252
  139.7 34.4 %shard_map.136 = f32[16,48,128]{2,1,0:T(8,128)} custom-call(f32[48,128]{1,0:T(8,128)} %reshape.1448.mine_ref), custom_call_target="tpu_custom_call" | custom-call | tf_op jit(solution)/shard_map/pallas_call | solution.py:52
  174.1 1.1 reshape.1449
  175.4 1.5 gather_fusion
  177.8 1.3 broadcast_select_fusion
  180.7 4.1 collective-permute-start.15
  184.8 1.4 fusion.refs_8_.refs_9_.refs_10_.refs_11_.refs_4_.refs_5_
  186.8 1.2 gather_fusion.1
  188.0 5.1 shard_map.137.refs_0_
  193.1 15.6 %shard_map.138.refs_4_ = bf16[4,160,2048]{2,1,0:T(8,128)(2,1)} custom-call(bf16[4,160,2048]{2,1,0:T(8,128)(2,1)} %shard_map.137.refs_0_, bf16[4,2048,1408]{2,1,0:T(8,128)(2,1)} %refs_1_.8, bf16[4,2048,1408]{2,1,0:T(8,128)(2,1)} %refs_2_.7, bf16[4,1408,2048]{2,1,0:T(8,128)(2,1)} %refs_3_.7), custom_call_target="tpu_custom_call" | custom-call | flops 5536481280 | bytes 34603008 | tf_op jit(solution)/shard_map/pallas_call | solution.py:119
  208.7 15.6 %shard_map.139.refs_0_ = bf16[4,160,2048]{2,1,0:T(8,128)(2,1)} custom-call(bf16[4,160,2048]{2,1,0:T(8,128)(2,1)} %shard_map.137.refs_0_, bf16[4,2048,1408]{2,1,0:T(8,128)(2,1)} %refs_1_.8, bf16[4,2048,1408]{2,1,0:T(8,128)(2,1)} %refs_2_.7, bf16[4,1408,2048]{2,1,0:T(8,128)(2,1)} %refs_3_.7, ...), custom_call_target="tpu_custom_call", output_to_operand_aliasing={{}: (4, {})} | custom-call | flops 5536481280 | bytes 34603008 | tf_op jit(solution)/shard_map/pallas_call | solution.py:119
  224.3 2.6 slice.32
  226.9 1.2 gather_fusion.2
  228.1 5.1 shard_map.140.refs_3_
  233.2 1.2 gather_fusion.3
  234.4 5.1 shard_map.141.refs_0_
  240.6 20.0 %shard_map.142.refs_4_ = bf16[4,320,2048]{2,1,0:T(8,128)(2,1)} custom-call(bf16[4,320,2048]{2,1,0:T(8,128)(2,1)} %shard_map.141.refs_0_, bf16[4,2048,1408]{2,1,0:T(8,128)(2,1)} %refs_1_.8, bf16[4,2048,1408]{2,1,0:T(8,128)(2,1)} %refs_2_.7, bf16[4,1408,2048]{2,1,0:T(8,128)(2,1)} %refs_3_.7), custom_call_target="tpu_custom_call" | custom-call | flops 11072962560 | bytes 34603008 | tf_op jit(solution)/shard_map/pallas_call | solution.py:119
  260.6 20.0 %shard_map.143.refs_2_ = bf16[4,320,2048]{2,1,0:T(8,128)(2,1)} custom-call(bf16[4,320,2048]{2,1,0:T(8,128)(2,1)} %shard_map.141.refs_0_, bf16[4,2048,1408]{2,1,0:T(8,128)(2,1)} %refs_1_.8, bf16[4,2048,1408]{2,1,0:T(8,128)(2,1)} %refs_2_.7, bf16[4,1408,2048]{2,1,0:T(8,128)(2,1)} %refs_3_.7, ...), custom_call_target="tpu_custom_call", output_to_operand_aliasing={{}: (4, {})} | custom-call | flops 11072962560 | bytes 34603008 | tf_op jit(solution)/shard_map/pallas_call | solution.py:119
  280.6 2.5 slice.33
  283.2 2.5 slice.34
  285.7 2.6 slice.35
  288.3 1.2 collective-permute-start.12
  289.5 0.9 collective-permute-start.10
  290.4 1.2 gather_fusion.4
  291.6 12.0 %shard_map.144.refs_0_ = bf16[4,480,2048]{2,1,0:T(8,128)(2,1)} custom-call(bf16[512,2048]{1,0:T(8,128)(2,1)} %collective-permute-done.15.refs_0_, bf16[512,2048]{1,0:T(8,128)(2,1)} %collective-permute-done.16.refs_1_, bf16[512,2048]{1,0:T(8,128)(2,1)} %collective-permute-done.14.refs_2_, bf16[512,2048]{1,0:T(8,128)(2,1)} %collective-permute-done.13.refs_3_, ...), custom_call_target="tpu_custom_call" | custom-call | flops 4026531840 | bytes 25165824 | tf_op jit(solution)/shard_map/pallas_call | solution.py:92
  303.6 11.5 %collective-permute-done.11.refs_1_ = bf16[4,80,2048]{2,1,0:T(8,128)(2,1)} collective-permute-done((bf16[4,80,2048]{2,1,0:T(8,128)(2,1)}, bf16[4,80,2048]{2,1,0:T(8,128)(2,1)}, u32[]{:S(2)}, u32[]{:S(2)}) %collective-permute-start.11) | collective-permute-done | bytes 1310752 | tf_op jit(solution)/shard_map/ppermute | solution.py:212
  315.1 3.2 collective-permute-done.10.refs_0_
  318.3 12.3 %shard_map.145 = f32[512,2048]{1,0:T(8,128)} custom-call(bf16[4,80,2048]{2,1,0:T(8,128)(2,1)} %collective-permute-done.10.refs_0_, bf16[4,80,2048]{2,1,0:T(8,128)(2,1)} %collective-permute-done.11.refs_1_, bf16[4,320,2048]{2,1,0:T(8,128)(2,1)} %shard_map.143.refs_2_, bf16[4,80,2048]{2,1,0:T(8,128)(2,1)} %collective-permute-done.12.refs_3_, ...), custom_call_target="tpu_custom_call" | custom-call | flops 8053063680 | bytes 4194304 | tf_op jit(solution)/shard_map/pallas_call | solution.py:180
  331.6 26.4 %shard_map.146.refs_4_ = bf16[4,480,2048]{2,1,0:T(8,128)(2,1)} custom-call(bf16[4,480,2048]{2,1,0:T(8,128)(2,1)} %shard_map.144.refs_0_, bf16[4,2048,1408]{2,1,0:T(8,128)(2,1)} %refs_1_.8, bf16[4,2048,1408]{2,1,0:T(8,128)(2,1)} %refs_2_.7, bf16[4,1408,2048]{2,1,0:T(8,128)(2,1)} %refs_3_.7), custom_call_target="tpu_custom_call" | custom-call | flops 16609443840 | bytes 34603008 | tf_op jit(solution)/shard_map/pallas_call | solution.py:119
  358.1 26.5 %shard_map.147.refs_2_.refs_0_ = bf16[4,480,2048]{2,1,0:T(8,128)(2,1)} custom-call(bf16[4,480,2048]{2,1,0:T(8,128)(2,1)} %shard_map.144.refs_0_, bf16[4,2048,1408]{2,1,0:T(8,128)(2,1)} %refs_1_.8, bf16[4,2048,1408]{2,1,0:T(8,128)(2,1)} %refs_2_.7, bf16[4,1408,2048]{2,1,0:T(8,128)(2,1)} %refs_3_.7, ...), custom_call_target="tpu_custom_call", output_to_operand_aliasing={{}: (4, {})} | custom-call | flops 16609443840 | bytes 34603008 | tf_op jit(solution)/shard_map/pallas_call | solution.py:119
  384.5 2.6 slice.36
  387.1 2.5 slice.37
  389.6 3.6 slice.38
  394.2 2.4 collective-permute-start.20
  396.6 8.5 %shard_map.148 = f32[512,2048]{1,0:T(8,128)} custom-call(bf16[4,160,2048]{2,1,0:T(8,128)(2,1)} %shard_map.139.refs_0_, bf16[4,80,2048]{2,1,0:T(8,128)(2,1)} %collective-permute-done.5.refs_1_, f32[28,4,512]{2,1,0:T(4,128)} %copy-done.2, f32[28,4,512]{2,1,0:T(4,128)} %copy-done.2, f32[28,4,512]{2,1,0:T(4,128)} %fusion.refs_8_.refs_9_.refs_10_.refs_11_.refs_4_.refs_5_, ...), custom_call_target="tpu_custom_call" | custom-call | flops 4026531840 | bytes 8388608 | tf_op jit(solution)/shard_map/pallas_call | solution.py:180
  405.1 2.1 gather_fusion.5
  407.2 8.5 %shard_map.149.refs_0_ = bf16[4,320,2048]{2,1,0:T(8,128)(2,1)} custom-call(bf16[512,2048]{1,0:T(8,128)(2,1)} %collective-permute-done.refs_0_, bf16[512,2048]{1,0:T(8,128)(2,1)} %refs_1_.6, bf16[512,2048]{1,0:T(8,128)(2,1)} %collective-permute-done.1.refs_2_, bf16[512,2048]{1,0:T(8,128)(2,1)} %collective-permute-done.2.refs_3_, f32[4,4,512]{2,1,0:T(4,128)} %gather_fusion.5), custom_call_target="tpu_custom_call" | custom-call | flops 2684354560 | bytes 16777216 | tf_op jit(solution)/shard_map/pallas_call | solution.py:92
  415.8 20.0 %shard_map.150.refs_4_ = bf16[4,320,2048]{2,1,0:T(8,128)(2,1)} custom-call(bf16[4,320,2048]{2,1,0:T(8,128)(2,1)} %shard_map.149.refs_0_, bf16[4,2048,1408]{2,1,0:T(8,128)(2,1)} %refs_1_.8, bf16[4,2048,1408]{2,1,0:T(8,128)(2,1)} %refs_2_.7, bf16[4,1408,2048]{2,1,0:T(8,128)(2,1)} %refs_3_.7), custom_call_target="tpu_custom_call" | custom-call | flops 11072962560 | bytes 34603008 | tf_op jit(solution)/shard_map/pallas_call | solution.py:119
  435.8 12.4 %shard_map.151 = f32[512,2048]{1,0:T(8,128)} custom-call(bf16[4,80,2048]{2,1,0:T(8,128)(2,1)} %collective-permute-done.20.refs_0_, bf16[4,80,2048]{2,1,0:T(8,128)(2,1)} %collective-permute-done.21.refs_1_, bf16[4,480,2048]{2,1,0:T(8,128)(2,1)} %shard_map.147.refs_2_.refs_0_, bf16[4,160,2048]{2,1,0:T(8,128)(2,1)} %collective-permute-done.22.refs_3_.refs_1_, ...), custom_call_target="tpu_custom_call" | custom-call | flops 8053063680 | bytes 4194304 | tf_op jit(solution)/shard_map/pallas_call | solution.py:180
  448.2 2.9 collective-permute-start.26
  451.1 19.9 %shard_map.152.refs_0_ = bf16[4,320,2048]{2,1,0:T(8,128)(2,1)} custom-call(bf16[4,320,2048]{2,1,0:T(8,128)(2,1)} %shard_map.149.refs_0_, bf16[4,2048,1408]{2,1,0:T(8,128)(2,1)} %refs_1_.8, bf16[4,2048,1408]{2,1,0:T(8,128)(2,1)} %refs_2_.7, bf16[4,1408,2048]{2,1,0:T(8,128)(2,1)} %refs_3_.7, ...), custom_call_target="tpu_custom_call", output_to_operand_aliasing={{}: (4, {})} | custom-call | flops 11072962560 | bytes 34603008 | tf_op jit(solution)/shard_map/pallas_call | solution.py:119
  471.0 2.1 slice.39
  473.1 0.8 collective-permute-start.23
  473.9 4.5 collective-permute-done.23.refs_1_
  478.4 1.5 copy-done.3
  479.9 8.1 %shard_map.153 = f32[512,2048]{1,0:T(8,128)} custom-call(bf16[4,320,2048]{2,1,0:T(8,128)(2,1)} %shard_map.152.refs_0_, bf16[4,160,2048]{2,1,0:T(8,128)(2,1)} %copy-done.3, f32[28,4,512]{2,1,0:T(4,128)} %copy-done.2, f32[28,4,512]{2,1,0:T(4,128)} %copy-done.2, f32[28,4,512]{2,1,0:T(4,128)} %fusion.refs_8_.refs_9_.refs_10_.refs_11_.refs_4_.refs_5_, ...), custom_call_target="tpu_custom_call" | custom-call | flops 4026531840 | bytes 8388608 | tf_op jit(solution)/shard_map/pallas_call | solution.py:180
  488.0 8.5 %shard_map.154 = f32[512,2048]{1,0:T(8,128)} custom-call(bf16[4,320,2048]{2,1,0:T(8,128)(2,1)} %shard_map.152.refs_0_, bf16[4,160,2048]{2,1,0:T(8,128)(2,1)} %copy-done.3, f32[28,4,512]{2,1,0:T(4,128)} %copy-done.2, f32[28,4,512]{2,1,0:T(4,128)} %copy-done.2, f32[28,4,512]{2,1,0:T(4,128)} %fusion.refs_8_.refs_9_.refs_10_.refs_11_.refs_4_.refs_5_, ...), custom_call_target="tpu_custom_call" | custom-call | flops 4026531840 | bytes 8388608 | tf_op jit(solution)/shard_map/pallas_call | solution.py:180
  496.5 18.9 %collective-permute-done.26.refs_6_ = f32[512,2048]{1,0:T(8,128)} collective-permute-done((f32[512,2048]{1,0:T(8,128)}, f32[512,2048]{1,0:T(8,128)}, u32[]{:S(2)}, u32[]{:S(2)}) %collective-permute-start.26) | collective-permute-done | bytes 4194336 | tf_op jit(solution)/shard_map/ppermute | solution.py:212
  515.4 8.5 %shard_map.155 = f32[512,2048]{1,0:T(8,128)} custom-call(bf16[4,480,2048]{2,1,0:T(8,128)(2,1)} %shard_map.147.refs_2_.refs_0_, bf16[4,160,2048]{2,1,0:T(8,128)(2,1)} %collective-permute-done.22.refs_3_.refs_1_, f32[28,4,512]{2,1,0:T(4,128)} %copy-done.2, f32[28,4,512]{2,1,0:T(4,128)} %copy-done.2, ...), custom_call_target="tpu_custom_call" | custom-call | flops 4026531840 | bytes 8388608 | tf_op jit(solution)/shard_map/pallas_call | solution.py:180
  523.8 3.1 collective-permute-start.27
  527.0 89.5 %collective-permute-done.27 = f32[512,2048]{1,0:T(8,128)S(1)} collective-permute-done((f32[512,2048]{1,0:T(8,128)}, f32[512,2048]{1,0:T(8,128)S(1)}, u32[]{:S(2)}, u32[]{:S(2)}) %collective-permute-start.27) | collective-permute-done | bytes 4194336 | tf_op jit(solution)/shard_map/ppermute | solution.py:212
  616.5 2.5 collective-permute-done.25
  618.9 4.8 add_convert_fusion
  (87 shorter events, 8.7 us)
Async XLA Ops:
  0.0 34.2 %copy-start = (bf16[2048,64]{0,1:T(8,128)(2,1)S(1)}, bf16[2048,64]{0,1:T(8,128)(2,1)}, u32[]{:S(2)}) copy-start(bf16[2048,64]{0,1:T(8,128)(2,1)} %param.15) | copy-start | bytes 786436
  0.0 82.5 %copy-start.4 = (bf16[512,2048]{1,0:T(8,128)(2,1)S(1)}, bf16[512,2048]{1,0:T(8,128)(2,1)}, u32[]{:S(2)}) copy-start(bf16[512,2048]{1,0:T(8,128)(2,1)} %refs_1_.6) | copy-start | bytes 6291460
  0.0 31.1 %collective-permute-start = (bf16[512,2048]{1,0:T(8,128)(2,1)}, bf16[512,2048]{1,0:T(8,128)(2,1)}, u32[]{:S(2)}, u32[]{:S(2)}) collective-permute-start(bf16[512,2048]{1,0:T(8,128)(2,1)} %refs_1_.6), channel_id=1, source_target_pairs={{0,2},{1,15},{2,4},{3,1},{4,6},{5,3},{6,8},{7,5},{8,10},{9,7},{10,... | collective-permute-start | bytes 6291464 | tf_op jit(solution)/shard_map/ppermute | solution.py:212
  31.1 46.6 %collective-permute-start.3 = (bf16[512,2048]{1,0:T(8,128)(2,1)}, bf16[512,2048]{1,0:T(8,128)(2,1)}, u32[]{:S(2)}, u32[]{:S(2)}) collective-permute-start(bf16[512,2048]{1,0:T(8,128)(2,1)} %collective-permute-done.refs_0_), channel_id=1, source_target_pairs={{0,2},{1,15},{2,4},{3,1},{4,6},{5,3},{6,8},{7,5},{8,10},{9,7},{10,... | collective-permute-start | bytes 6291464 | tf_op jit(solution)/shard_map/ppermute | solution.py:212
  34.2 83.1 %collective-permute-start.13 = (bf16[512,2048]{1,0:T(8,128)(2,1)}, bf16[512,2048]{1,0:T(8,128)(2,1)}, u32[]{:S(2)}, u32[]{:S(2)}) collective-permute-start(bf16[512,2048]{1,0:T(8,128)(2,1)} %refs_1_.6), channel_id=1, source_target_pairs={{2,0},{15,1},{4,2},{1,3},{6,4},{3,5},{8,6},{5,7},{10,8},{7,9},{12,... | collective-permute-start | bytes 6291464 | tf_op jit(solution)/shard_map/ppermute | solution.py:212
  77.7 26.7 %collective-permute-start.6 = (bf16[512,2048]{1,0:T(8,128)(2,1)}, bf16[512,2048]{1,0:T(8,128)(2,1)}, u32[]{:S(2)}, u32[]{:S(2)}) collective-permute-start(bf16[512,2048]{1,0:T(8,128)(2,1)} %collective-permute-done.3.refs_0_), channel_id=1, source_target_pairs={{0,2},{1,15},{2,4},{3,1},{4,6},{5,3},{6,8},{7,5},{8,10},{9,7},{10,... | collective-permute-start | bytes 6291464 | tf_op jit(solution)/shard_map/ppermute | solution.py:212
  82.5 25.0 %copy-start.10 = (bf16[2048,2816]{1,0:T(8,128)(2,1)S(1)}, bf16[2048,2816]{1,0:T(8,128)(2,1)}, u32[]{:S(2)}) copy-start(bf16[2048,2816]{1,0:T(8,128)(2,1)} %param.21) | copy-start | bytes 34603012
  82.5 48.3 %slice-start = ((s8[11534336]{0:T(1024)(128)(4,1)}), s8[4194304]{0:T(1024)(128)(4,1)S(1)}, s32[]{:S(2)}) async-start(s8[11534336]{0:T(1024)(128)(4,1)} %bitcast.52), calls=%async_computation | async-start | bytes 8388608
  82.5 48.3 %slice-start.1 = ((s8[11534336]{0:T(1024)(128)(4,1)}), s8[4194304]{0:T(1024)(128)(4,1)S(1)}, s32[]{:S(2)}) async-start(s8[11534336]{0:T(1024)(128)(4,1)} %bitcast.52), calls=%async_computation.1 | async-start | bytes 8388608
  93.8 37.1 %slice-start.2 = ((s8[11534336]{0:T(1024)(128)(4,1)}), s8[3145728]{0:T(1024)(128)(4,1)S(1)}, s32[]{:S(2)}) async-start(s8[11534336]{0:T(1024)(128)(4,1)} %bitcast.52), calls=%async_computation.2 | async-start | bytes 6291456
  104.4 26.4 %collective-permute-start.7 = (bf16[512,2048]{1,0:T(8,128)(2,1)}, bf16[512,2048]{1,0:T(8,128)(2,1)}, u32[]{:S(2)}, u32[]{:S(2)}) collective-permute-start(bf16[512,2048]{1,0:T(8,128)(2,1)} %collective-permute-done.6.refs_0_), channel_id=1, source_target_pairs={{0,2},{1,15},{2,4},{3,1},{4,6},{5,3},{6,8},{7,5},{8,10},{9,7},{10,... | collective-permute-start | bytes 6291464 | tf_op jit(solution)/shard_map/ppermute | solution.py:212
  130.9 49.8 %collective-permute-start.14 = (bf16[512,2048]{1,0:T(8,128)(2,1)}, bf16[512,2048]{1,0:T(8,128)(2,1)}, u32[]{:S(2)}, u32[]{:S(2)}) collective-permute-start(bf16[512,2048]{1,0:T(8,128)(2,1)} %collective-permute-done.13.refs_3_), channel_id=1, source_target_pairs={{2,0},{15,1},{4,2},{1,3},{6,4},{3,5},{8,6},{5,7},{10,8},{7,9},{12,... | collective-permute-start | bytes 6291464 | tf_op jit(solution)/shard_map/ppermute | solution.py:212
  175.4 4.8 copy-start.9
  175.4 5.3 copy-start.8
  175.4 9.4 %copy-start.7 = (s32[2]{0:T(128)S(1)}, s32[2]{0:T(128)}, u32[]{:S(2)}) copy-start(s32[2]{0:T(128)} %constant.229) | copy-start | bytes 28
  177.2 9.6 %collective-permute-start.4 = (bf16[512,2048]{1,0:T(8,128)(2,1)}, bf16[512,2048]{1,0:T(8,128)(2,1)}, u32[]{:S(2)}, u32[]{:S(2)}) collective-permute-start(bf16[512,2048]{1,0:T(8,128)(2,1)} %collective-permute-done.3.refs_0_), channel_id=1, source_target_pairs={{0,1},{1,0},{2,3},{3,2},{4,5},{5,4},{6,7},{7,6},{8,9},{9,8},{10,11... | collective-permute-start | bytes 6291464 | tf_op jit(solution)/shard_map/ppermute | solution.py:212
  179.7 47.2 %collective-permute-start.9 = (bf16[512,2048]{1,0:T(8,128)(2,1)}, bf16[512,2048]{1,0:T(8,128)(2,1)}, u32[]{:S(2)}, u32[]{:S(2)}) collective-permute-start(bf16[512,2048]{1,0:T(8,128)(2,1)} %collective-permute-done.6.refs_0_), channel_id=1, source_target_pairs={{0,1},{1,0},{2,3},{3,2},{4,5},{5,4},{6,7},{7,6},{8,9},{9,8},{10,11... | collective-permute-start | bytes 6291464 | tf_op jit(solution)/shard_map/ppermute | solution.py:212
  180.2 53.0 %collective-permute-start.8 = (bf16[512,2048]{1,0:T(8,128)(2,1)}, bf16[512,2048]{1,0:T(8,128)(2,1)}, u32[]{:S(2)}, u32[]{:S(2)}) collective-permute-start(bf16[512,2048]{1,0:T(8,128)(2,1)} %collective-permute-done.7.refs_0_), channel_id=1, source_target_pairs={{0,1},{1,0},{2,3},{3,2},{4,5},{5,4},{6,7},{7,6},{8,9},{9,8},{10,11... | collective-permute-start | bytes 6291464 | tf_op jit(solution)/shard_map/ppermute | solution.py:212
  180.7 59.4 %collective-permute-start.15 = (bf16[512,2048]{1,0:T(8,128)(2,1)}, bf16[512,2048]{1,0:T(8,128)(2,1)}, u32[]{:S(2)}, u32[]{:S(2)}) collective-permute-start(bf16[512,2048]{1,0:T(8,128)(2,1)} %collective-permute-done.14.refs_2_), channel_id=1, source_target_pairs={{2,0},{15,1},{4,2},{1,3},{6,4},{3,5},{8,6},{5,7},{10,8},{7,9},{12,... | collective-permute-start | bytes 6291464 | tf_op jit(solution)/shard_map/ppermute | solution.py:212
  186.7 103.7 %copy-start.2 = (f32[28,4,512]{2,1,0:T(4,128)}, f32[28,4,512]{2,1,0:T(4,128)S(1)}, u32[]{:S(2)}) copy-start(f32[28,4,512]{2,1,0:T(4,128)S(1)} %copy_select_fusion.refs_4_.refs_5_.refs_6_.refs_7_.refs_2_.refs_3_) | copy-start | bytes 688132
  186.7 102.8 %collective-permute-start.18 = (bf16[512,2048]{1,0:T(8,128)(2,1)}, bf16[512,2048]{1,0:T(8,128)(2,1)}, u32[]{:S(2)}, u32[]{:S(2)}) collective-permute-start(bf16[512,2048]{1,0:T(8,128)(2,1)} %collective-permute-done.13.refs_3_), channel_id=1, source_target_pairs={{0,1},{1,0},{2,3},{3,2},{4,5},{5,4},{6,7},{7,6},{8,9},{9,8},{10,11... | collective-permute-start | bytes 6291464 | tf_op jit(solution)/shard_map/ppermute | solution.py:212
  239.5 50.9 %collective-permute-start.17 = (bf16[512,2048]{1,0:T(8,128)(2,1)}, bf16[512,2048]{1,0:T(8,128)(2,1)}, u32[]{:S(2)}, u32[]{:S(2)}) collective-permute-start(bf16[512,2048]{1,0:T(8,128)(2,1)} %collective-permute-done.14.refs_2_), channel_id=1, source_target_pairs={{0,1},{1,0},{2,3},{3,2},{4,5},{5,4},{6,7},{7,6},{8,9},{9,8},{10,11... | collective-permute-start | bytes 6291464 | tf_op jit(solution)/shard_map/ppermute | solution.py:212
  240.1 50.3 %collective-permute-start.16 = (bf16[512,2048]{1,0:T(8,128)(2,1)}, bf16[512,2048]{1,0:T(8,128)(2,1)}, u32[]{:S(2)}, u32[]{:S(2)}) collective-permute-start(bf16[512,2048]{1,0:T(8,128)(2,1)} %collective-permute-done.15.refs_0_), channel_id=1, source_target_pairs={{0,1},{1,0},{2,3},{3,2},{4,5},{5,4},{6,7},{7,6},{8,9},{9,8},{10,11... | collective-permute-start | bytes 6291464 | tf_op jit(solution)/shard_map/ppermute | solution.py:212
  283.2 7.2 %copy-start.6 = (s32[6]{0:T(128)S(1)}, s32[6]{0:T(128)}, u32[]{:S(2)}) copy-start(s32[6]{0:T(128)} %constant.230) | copy-start | bytes 76
  285.7 29.4 %collective-permute-start.11 = (bf16[4,80,2048]{2,1,0:T(8,128)(2,1)}, bf16[4,80,2048]{2,1,0:T(8,128)(2,1)}, u32[]{:S(2)}, u32[]{:S(2)}) collective-permute-start(bf16[4,80,2048]{2,1,0:T(8,128)(2,1)} %slice.34), channel_id=1, source_target_pairs={{0,3},{1,14},{2,5},{3,0},{4,7},{5,2},{6,9},{7,4},{8,11},{9,6},{10,... | collective-permute-start | bytes 3932168 | tf_op jit(solution)/shard_map/ppermute | solution.py:212
  288.3 15.3 %collective-permute-start.12 = (bf16[4,80,2048]{2,1,0:T(8,128)(2,1)}, bf16[4,80,2048]{2,1,0:T(8,128)(2,1)}, u32[]{:S(2)}, u32[]{:S(2)}) collective-permute-start(bf16[4,80,2048]{2,1,0:T(8,128)(2,1)} %slice.35), channel_id=1, source_target_pairs={{0,1},{1,0},{2,3},{3,2},{4,5},{5,4},{6,7},{7,6},{8,9},{9,8},{10,11... | collective-permute-start | bytes 3932168 | tf_op jit(solution)/shard_map/ppermute | solution.py:212
  289.5 28.8 %collective-permute-start.10 = (bf16[4,80,2048]{2,1,0:T(8,128)(2,1)}, bf16[4,80,2048]{2,1,0:T(8,128)(2,1)}, u32[]{:S(2)}, u32[]{:S(2)}) collective-permute-start(bf16[4,80,2048]{2,1,0:T(8,128)(2,1)} %slice.33), channel_id=1, source_target_pairs={{2,0},{15,1},{4,2},{1,3},{6,4},{3,5},{8,6},{5,7},{10,8},{7,9},{12,... | collective-permute-start | bytes 3932168 | tf_op jit(solution)/shard_map/ppermute | solution.py:212
  330.6 63.6 %collective-permute-start.19 = (f32[512,2048]{1,0:T(8,128)}, f32[512,2048]{1,0:T(8,128)}, u32[]{:S(2)}, u32[]{:S(2)}) collective-permute-start(f32[512,2048]{1,0:T(8,128)} %shard_map.145), channel_id=1, source_target_pairs={{2,0},{15,1},{4,2},{1,3},{6,4},{3,5},{8,6},{5,7},{10,8},{7,9},{12,... | collective-permute-start | bytes 12582920 | tf_op jit(solution)/shard_map/ppermute | solution.py:212
  330.6 74.5 %collective-permute-start.2 = (bf16[512,2048]{1,0:T(8,128)(2,1)S(1)}, bf16[512,2048]{1,0:T(8,128)(2,1)}, u32[]{:S(2)}, u32[]{:S(2)}) collective-permute-start(bf16[512,2048]{1,0:T(8,128)(2,1)S(1)} %copy-done.4), channel_id=1, source_target_pairs={{0,1},{1,0},{2,3},{3,2},{4,5},{5,4},{6,7},{7,6},{8,9},{9,8},{10,11... | collective-permute-start | bytes 6291464 | tf_op jit(solution)/shard_map/ppermute | solution.py:212
  331.0 74.1 %collective-permute-start.1 = (bf16[512,2048]{1,0:T(8,128)(2,1)}, bf16[512,2048]{1,0:T(8,128)(2,1)}, u32[]{:S(2)}, u32[]{:S(2)}) collective-permute-start(bf16[512,2048]{1,0:T(8,128)(2,1)} %collective-permute-done.refs_0_), channel_id=1, source_target_pairs={{0,1},{1,0},{2,3},{3,2},{4,5},{5,4},{6,7},{7,6},{8,9},{9,8},{10,11... | collective-permute-start | bytes 6291464 | tf_op jit(solution)/shard_map/ppermute | solution.py:212
  331.2 62.2 %collective-permute-start.5 = (bf16[4,80,2048]{2,1,0:T(8,128)(2,1)}, bf16[4,80,2048]{2,1,0:T(8,128)(2,1)}, u32[]{:S(2)}, u32[]{:S(2)}) collective-permute-start(bf16[4,80,2048]{2,1,0:T(8,128)(2,1)} %slice.32), channel_id=1, source_target_pairs={{0,1},{1,0},{2,3},{3,2},{4,5},{5,4},{6,7},{7,6},{8,9},{9,8},{10,11... | collective-permute-start | bytes 3932168 | tf_op jit(solution)/shard_map/ppermute | solution.py:212
  389.6 3.8 copy-start.5
  393.2 42.6 %collective-permute-start.22 = (bf16[4,160,2048]{2,1,0:T(8,128)(2,1)}, bf16[4,160,2048]{2,1,0:T(8,128)(2,1)}, u32[]{:S(2)}, u32[]{:S(2)}) collective-permute-start(bf16[4,160,2048]{2,1,0:T(8,128)(2,1)} %slice.38), channel_id=1, source_target_pairs={{0,1},{1,0},{2,3},{3,2},{4,5},{5,4},{6,7},{7,6},{8,9},{9,8},{10,11... | collective-permute-start | bytes 7864328 | tf_op jit(solution)/shard_map/ppermute | solution.py:212
  393.4 42.3 %collective-permute-start.21 = (bf16[4,80,2048]{2,1,0:T(8,128)(2,1)}, bf16[4,80,2048]{2,1,0:T(8,128)(2,1)}, u32[]{:S(2)}, u32[]{:S(2)}) collective-permute-start(bf16[4,80,2048]{2,1,0:T(8,128)(2,1)} %slice.37), channel_id=1, source_target_pairs={{2,1},{15,0},{4,3},{1,2},{6,5},{3,4},{8,7},{5,6},{10,9},{7,8},{12,... | collective-permute-start | bytes 3932168 | tf_op jit(solution)/shard_map/ppermute | solution.py:212
  394.2 41.6 %collective-permute-start.20 = (bf16[4,80,2048]{2,1,0:T(8,128)(2,1)}, bf16[4,80,2048]{2,1,0:T(8,128)(2,1)}, u32[]{:S(2)}, u32[]{:S(2)}) collective-permute-start(bf16[4,80,2048]{2,1,0:T(8,128)(2,1)} %slice.36), channel_id=1, source_target_pairs={{0,2},{1,15},{2,4},{3,1},{4,6},{5,3},{6,8},{7,5},{8,10},{9,7},{10,... | collective-permute-start | bytes 3932168 | tf_op jit(solution)/shard_map/ppermute | solution.py:212
  405.1 82.9 %collective-permute-start.24 = (f32[512,2048]{1,0:T(8,128)}, f32[512,2048]{1,0:T(8,128)}, u32[]{:S(2)}, u32[]{:S(2)}) collective-permute-start(f32[512,2048]{1,0:T(8,128)} %shard_map.148), channel_id=1, source_target_pairs={{2,0},{15,1},{4,2},{1,3},{6,4},{3,5},{8,6},{5,7},{10,8},{7,9},{12,... | collective-permute-start | bytes 12582920 | tf_op jit(solution)/shard_map/ppermute | solution.py:212
  448.2 67.2 %collective-permute-start.26 = (f32[512,2048]{1,0:T(8,128)}, f32[512,2048]{1,0:T(8,128)}, u32[]{:S(2)}, u32[]{:S(2)}) collective-permute-start(f32[512,2048]{1,0:T(8,128)} %shard_map.151), channel_id=1, source_target_pairs={{0,2},{1,15},{2,4},{3,1},{4,6},{5,3},{6,8},{7,5},{8,10},{9,7},{10,... | collective-permute-start | bytes 12582920 | tf_op jit(solution)/shard_map/ppermute | solution.py:212
  473.1 5.4 collective-permute-start.23
  478.4 1.5 copy-start.3
  523.8 92.6 %collective-permute-start.27 = (f32[512,2048]{1,0:T(8,128)}, f32[512,2048]{1,0:T(8,128)S(1)}, u32[]{:S(2)}, u32[]{:S(2)}) collective-permute-start(f32[512,2048]{1,0:T(8,128)} %shard_map.155), channel_id=1, source_target_pairs={{0,2},{1,15},{2,4},{3,1},{4,6},{5,3},{6,8},{7,5},{8,10},{9,7},{10,... | collective-permute-start | bytes 12582920 | tf_op jit(solution)/shard_map/ppermute | solution.py:212
  527.0 92.0 %collective-permute-start.25 = (f32[512,2048]{1,0:T(8,128)}, f32[512,2048]{1,0:T(8,128)S(1)}, u32[]{:S(2)}, u32[]{:S(2)}) collective-permute-start(f32[512,2048]{1,0:T(8,128)} %shard_map.154), channel_id=1, source_target_pairs={{2,0},{15,1},{4,2},{1,3},{6,4},{3,5},{8,6},{5,7},{10,8},{7,9},{12,... | collective-permute-start | bytes 12582920 | tf_op jit(solution)/shard_map/ppermute | solution.py:212
  618.9 4.8 copy-start.1
where the time goes:
time: 633 us; the launch traced here: 624 us
  Pallas kernels  293 us (46%)
  waiting for transfers between devices  218 us (34%)
  starting transfers between devices  37.7 us (6%)
  local copies, waits for them, and re-layouts  32.8 us (5%)
  matrix products  32.4 us (5%)
  other arithmetic  10 us (2%)
    ppermute x28, waiting for transfers between devices, send(): return lax.ppermute(value, 'ep', perms[way])  218 us
    pallas_call x8, Pallas kernels, expert_mlp(): pl.pallas_call(expert_kernel, grid=(count,), out_shape=jax.ShapeDtypeStru...  164 us
    pallas_call x6, Pallas kernels, combine_rows(): pl.pallas_call(functools.partial(combine_kernel, len(pieces), len(added))...  58.2 us
    ppermute x28, starting transfers between devices, send(): return lax.ppermute(value, 'ep', perms[way])  37.7 us
    pallas_call x5, Pallas kernels, dispatch_rows(): pl.pallas_call(functools.partial(dispatch_kernel, count, slots), grid=(co...  35.8 us
    pallas_call x1, Pallas kernels, exchange(): pl.pallas_call(functools.partial(exchange_kernel, group), out_shape=jax.S...  34.4 us
    slice x8, local copies, waits for them, and re-layouts, blocks(): return step(lambda o: o[:, start * slots:stop * slots], out)  20.9 us
  transfers between devices with their start and end apart: 28, of which 10 were waited for; matrix products, arithmetic and copies ran while one was open for 11% of the time, Pallas kernels for 44%

commit v1 on v0

--- a/solution.py
+++ b/solution.py
@@ -323,8 +323,8 @@
 
         names_0 = [('a', 2, False), ('a', 2, True)]
         names_1 = [('a', far, False), ('a', far, True), ('a', 3, False), ('a', 3, True)]
-        names_2 = [('a', 1, False), ('a', 0, False), ('a', 1, True), ('a', 0, True)]
-        names_3 = [('b', 3, False), ('b', 3, True), ('b', 2, False), ('b', 1, False), ('b', 2, True), ('b', 1, True)]
+        names_2 = [('a', 1, False), ('a', 0, False), ('b', 1, False), ('a', 1, True), ('a', 0, True), ('b', 1, True)]
+        names_3 = [('b', 3, False), ('b', 3, True), ('b', 2, False), ('b', 2, True)]
 
         a_oth = [send('swap', tok_rows)] + [send('swap', a_own[d]) for d in range(1, far)]
         b_oth = [None, send('swap', b_own[1])]
@@ -347,22 +347,22 @@
         oth_1 = send('swap', blocks(out_1, 3, 4))
         b_oth.append(send('swap', b_own[3]))
 
-        rows_3 = gather_rows(names_3, 0, 6)
+        rows_3 = gather_rows(names_3, 0, 4)
+        rows_2 = gather_rows(names_2, 0, 6)
         acc_a = send('back', total([(got_own, 0, ('ra', False)), (got_oth, 0, ('ra', True)), (out_1, 2, ('a', 3, False)), (oth_1, 0, ('sa', 3))]))
         out_3 = mlp_first(rows_3)
         out_3 = mlp_rest(rows_3, out_3)
         got_own = send('away', blocks(out_3, 0, 1))
         got_oth = send('back_cross', blocks(out_3, 1, 2))
-        oth_3 = send('swap', blocks(out_3, 4, 6))
+        oth_3 = send('swap', blocks(out_3, 3, 4))
         acc_a = send('back', total([(out_0, 0, ('a', 2, False)), (oth_0, 0, ('sa', 2))], [acc_a]))
-        rows_2 = gather_rows(names_2, 0, 4)
         out_2 = mlp_first(rows_2)
         acc_b = send('away', total([(got_own, 0, ('rb', False)), (got_oth, 0, ('rb', True)), (out_3, 2, ('b', 2, False)), (oth_3, 0, ('sb', 2))]))
         out_2 = mlp_rest(rows_2, out_2)
-        oth_2 = send('swap', blocks(out_2, 2, 4))
+        oth_2 = send('swap', blocks(out_2, 3, 6))
+        acc_a = send('back', total([(out_2, 0, ('a', 1, False)), (oth_2, 0, ('sa', 1))], [acc_a]))
+        acc_b = send('away', total([(out_2, 2, ('b', 1, False)), (oth_2, 2, ('sb', 1))], [acc_b]))
         here = total([(out_2, 1, ('a', 0, False)), (oth_2, 1, ('sa', 0))], [shared_out])
-        acc_a = send('back', total([(out_2, 0, ('a', 1, False)), (oth_2, 0, ('sa', 1))], [acc_a]))
-        acc_b = send('away', total([(out_3, 3, ('b', 1, False)), (oth_3, 1, ('sb', 1))], [acc_b]))
         return step(lambda x, a, b: (x + a + b).astype(jnp.bfloat16), here, acc_a, acc_b)
 
 

time: 633 us -> 628 us (level)
  transfers between devices with their start and end apart: 28 -> 28, of which waited for: 10 -> 10; matrix products, arithmetic and copies ran while one was open for 11% -> 10% of each run, Pallas kernels for 44% -> 44%
where the time goes in v1:
time: 628 us; the launch traced here: 618 us
  Pallas kernels  292 us (46%)
  waiting for transfers between devices  216 us (34%)
  starting transfers between devices  36.8 us (6%)
  matrix products  33.1 us (5%)
  local copies, waits for them, and re-layouts  27.7 us (4%)
  other arithmetic  11.2 us (2%)
    ppermute x28, waiting for transfers between devices, send(): return lax.ppermute(value, 'ep', perms[way])  216 us
    pallas_call x8, Pallas kernels, expert_mlp(): pl.pallas_call(expert_kernel, grid=(count,), out_shape=jax.ShapeDtypeStru...  164 us
    pallas_call x6, Pallas kernels, combine_rows(): pl.pallas_call(functools.partial(combine_kernel, len(pieces), len(added))...  58.4 us
    ppermute x28, starting transfers between devices, send(): return lax.ppermute(value, 'ep', perms[way])  36.8 us
    pallas_call x5, Pallas kernels, dispatch_rows(): pl.pallas_call(functools.partial(dispatch_kernel, count, slots), grid=(co...  35.8 us
    pallas_call x1, Pallas kernels, exchange(): pl.pallas_call(functools.partial(exchange_kernel, group), out_shape=jax.S...  33.7 us
    slice x8, local copies, waits for them, and re-layouts, blocks(): return step(lambda o: o[:, start * slots:stop * slots], out)  19 us
  transfers between devices with their start and end apart: 28, of which 10 were waited for; matrix products, arithmetic and copies ran while one was open for 10% of the time, Pallas kernels for 44%

profile of v1, /device:TPU:21, one launch (start us, length us, event | category | flops | bytes accessed | tf_op | source)
XLA Modules:
  0.0 618.2 jit_solution(10626152006702826919)
XLA Ops:
  0.0 7.8 %collective-permute-start = (bf16[512,2048]{1,0:T(8,128)(2,1)}, bf16[512,2048]{1,0:T(8,128)(2,1)}, u32[]{:S(2)}, u32[]{:S(2)}) collective-permute-start(bf16[512,2048]{1,0:T(8,128)(2,1)} %refs_1_.4), channel_id=1, source_target_pairs={{0,2},{1,15},{2,4},{3,1},{4,6},{5,3},{6,8},{7,5},{8,10},{9,7},{10,... | collective-permute-start | bytes 6291464 | tf_op jit(solution)/shard_map/ppermute | solution.py:212
  7.8 23.3 %collective-permute-done.refs_0_ = bf16[512,2048]{1,0:T(8,128)(2,1)} collective-permute-done((bf16[512,2048]{1,0:T(8,128)(2,1)}, bf16[512,2048]{1,0:T(8,128)(2,1)}, u32[]{:S(2)}, u32[]{:S(2)}) %collective-permute-start) | collective-permute-done | bytes 2097184 | tf_op jit(solution)/shard_map/ppermute | solution.py:212
  31.1 3.1 collective-permute-start.5
  34.2 2.1 collective-permute-start.3
  36.3 2.3 fusion.8
  38.7 0.8 select_reduce_fusion
  39.5 38.2 %collective-permute-done.5.refs_0_ = bf16[512,2048]{1,0:T(8,128)(2,1)} collective-permute-done((bf16[512,2048]{1,0:T(8,128)(2,1)}, bf16[512,2048]{1,0:T(8,128)(2,1)}, u32[]{:S(2)}, u32[]{:S(2)}) %collective-permute-start.5) | collective-permute-done | bytes 2097184 | tf_op jit(solution)/shard_map/ppermute | solution.py:212
  77.7 3.4 collective-permute-start.6
  81.2 0.7 convert_bitcast_fusion
  82.5 11.3 %fusion.9 = f32[512,2816]{1,0:T(8,128)} fusion(bf16[512,2048]{1,0:T(8,128)(2,1)S(1)} %copy-done.3, bf16[2048,2816]{1,0:T(8,128)(2,1)} %param.20), kind=kOutput, calls=%fused_computation.40 | convolution fusion | flops 5905580032 | bytes 19398656 | tf_op jit(solution)/shard_map/dot_general | solution.py:245
  93.8 10.6 %collective-permute-done.6.refs_0_ = bf16[512,2048]{1,0:T(8,128)(2,1)} collective-permute-done((bf16[512,2048]{1,0:T(8,128)(2,1)}, bf16[512,2048]{1,0:T(8,128)(2,1)}, u32[]{:S(2)}, u32[]{:S(2)}) %collective-permute-start.6) | collective-permute-done | bytes 2097184 | tf_op jit(solution)/shard_map/ppermute | solution.py:212
  104.4 3.1 collective-permute-start.7
  107.6 9.7 %multiply_convert_fusion = bf16[512,2816]{1,0:T(8,128)(2,1)} fusion(f32[512,2816]{1,0:T(8,128)} %fusion.9, bf16[512,2048]{1,0:T(8,128)(2,1)S(1)} %copy-done.3, bf16[2048,2816]{1,0:T(8,128)(2,1)S(1)} %copy-done.12), kind=kOutput, calls=%fused_computation.6 | convolution fusion | flops 5914230784 | bytes 22282240 | tf_op jit(solution)/shard_map/dot_general | solution.py:248
  117.2 13.6 %collective-permute-done.7.refs_0_ = bf16[512,2048]{1,0:T(8,128)(2,1)S(1)} collective-permute-done((bf16[512,2048]{1,0:T(8,128)(2,1)}, bf16[512,2048]{1,0:T(8,128)(2,1)S(1)}, u32[]{:S(2)}, u32[]{:S(2)}) %collective-permute-start.7) | collective-permute-done | bytes 2097184 | tf_op jit(solution)/shard_map/ppermute | solution.py:212
  130.9 9.6 %convolution_convert_fusion.refs_6_ = bf16[512,2048]{1,0:T(8,128)(2,1)} fusion(bf16[512,2816]{1,0:T(8,128)(2,1)} %multiply_convert_fusion, bf16[2816,2048]{1,0:T(8,128)(2,1)S(1)} %bitcast.53), kind=kOutput, calls=%fused_computation.8 | convolution fusion | flops 5906628608 | bytes 16515072 | tf_op jit(solution)/shard_map/dot_general | solution.py:252
  140.5 33.7 %shard_map.136 = f32[16,48,128]{2,1,0:T(8,128)} custom-call(f32[48,128]{1,0:T(8,128)} %reshape.1448.mine_ref), custom_call_target="tpu_custom_call" | custom-call | tf_op jit(solution)/shard_map/pallas_call | solution.py:52
  174.1 1.1 reshape.1449
  176.3 0.7 collective-permute-start.14
  178.6 4.0 collective-permute-start.9
  182.6 1.4 fusion.refs_8_.refs_9_.refs_10_.refs_11_.refs_4_.refs_5_
  184.7 1.2 gather_fusion.1
  185.8 5.1 shard_map.137.refs_0_
  191.0 15.6 %shard_map.138.refs_4_ = bf16[4,160,2048]{2,1,0:T(8,128)(2,1)} custom-call(bf16[4,160,2048]{2,1,0:T(8,128)(2,1)} %shard_map.137.refs_0_, bf16[4,2048,1408]{2,1,0:T(8,128)(2,1)} %refs_1_.8, bf16[4,2048,1408]{2,1,0:T(8,128)(2,1)} %refs_2_.7, bf16[4,1408,2048]{2,1,0:T(8,128)(2,1)} %refs_3_.7), custom_call_target="tpu_custom_call" | custom-call | flops 5536481280 | bytes 34603008 | tf_op jit(solution)/shard_map/pallas_call | solution.py:119
  206.6 15.6 %shard_map.139.refs_0_ = bf16[4,160,2048]{2,1,0:T(8,128)(2,1)} custom-call(bf16[4,160,2048]{2,1,0:T(8,128)(2,1)} %shard_map.137.refs_0_, bf16[4,2048,1408]{2,1,0:T(8,128)(2,1)} %refs_1_.8, bf16[4,2048,1408]{2,1,0:T(8,128)(2,1)} %refs_2_.7, bf16[4,1408,2048]{2,1,0:T(8,128)(2,1)} %refs_3_.7, ...), custom_call_target="tpu_custom_call", output_to_operand_aliasing={{}: (4, {})} | custom-call | flops 5536481280 | bytes 34603008 | tf_op jit(solution)/shard_map/pallas_call | solution.py:119
  222.2 2.5 slice.32
  225.2 1.2 gather_fusion.2
  226.4 5.1 shard_map.140.refs_3_
  231.5 1.2 gather_fusion.3
  232.7 0.9 collective-permute-start.10
  233.6 5.1 shard_map.141.refs_0_
  238.7 20.0 %shard_map.142.refs_4_ = bf16[4,320,2048]{2,1,0:T(8,128)(2,1)} custom-call(bf16[4,320,2048]{2,1,0:T(8,128)(2,1)} %shard_map.141.refs_0_, bf16[4,2048,1408]{2,1,0:T(8,128)(2,1)} %refs_1_.8, bf16[4,2048,1408]{2,1,0:T(8,128)(2,1)} %refs_2_.7, bf16[4,1408,2048]{2,1,0:T(8,128)(2,1)} %refs_3_.7), custom_call_target="tpu_custom_call" | custom-call | flops 11072962560 | bytes 34603008 | tf_op jit(solution)/shard_map/pallas_call | solution.py:119
  258.7 20.0 %shard_map.143.refs_2_ = bf16[4,320,2048]{2,1,0:T(8,128)(2,1)} custom-call(bf16[4,320,2048]{2,1,0:T(8,128)(2,1)} %shard_map.141.refs_0_, bf16[4,2048,1408]{2,1,0:T(8,128)(2,1)} %refs_1_.8, bf16[4,2048,1408]{2,1,0:T(8,128)(2,1)} %refs_2_.7, bf16[4,1408,2048]{2,1,0:T(8,128)(2,1)} %refs_3_.7, ...), custom_call_target="tpu_custom_call", output_to_operand_aliasing={{}: (4, {})} | custom-call | flops 11072962560 | bytes 34603008 | tf_op jit(solution)/shard_map/pallas_call | solution.py:119
  278.7 2.5 slice.33
  281.2 2.5 slice.34
  283.8 2.5 slice.35
  286.3 1.2 collective-permute-start.18
  287.5 0.8 collective-permute-start.16
  288.3 1.2 gather_fusion.4
  289.5 8.5 %shard_map.144.refs_0_ = bf16[4,320,2048]{2,1,0:T(8,128)(2,1)} custom-call(bf16[512,2048]{1,0:T(8,128)(2,1)} %collective-permute-done.9.refs_0_, bf16[512,2048]{1,0:T(8,128)(2,1)} %collective-permute-done.10.refs_1_, bf16[512,2048]{1,0:T(8,128)(2,1)} %collective-permute-done.8.refs_2_, bf16[512,2048]{1,0:T(8,128)(2,1)} %collective-permute-done.11.refs_3_, ...), custom_call_target="tpu_custom_call" | custom-call | flops 2684354560 | bytes 16777216 | tf_op jit(solution)/shard_map/pallas_call | solution.py:92
  298.1 1.3 gather_fusion.5
  299.4 12.0 %shard_map.145.refs_0_ = bf16[4,480,2048]{2,1,0:T(8,128)(2,1)} custom-call(bf16[512,2048]{1,0:T(8,128)(2,1)} %collective-permute-done.refs_0_, bf16[512,2048]{1,0:T(8,128)(2,1)} %refs_1_.4, bf16[512,2048]{1,0:T(8,128)(2,1)} %collective-permute-done.1.refs_2_, bf16[512,2048]{1,0:T(8,128)(2,1)} %copy-done.4, bf16[512,2048]{1,0:T(8,128)(2,1)} %collective-permute-done.3.refs_4_, ...), custom_call_target="tpu_custom_call" | custom-call | flops 4026531840 | bytes 25165824 | tf_op jit(solution)/shard_map/pallas_call | solution.py:92
  311.4 6.9 %collective-permute-done.17.refs_1_ = bf16[4,80,2048]{2,1,0:T(8,128)(2,1)} collective-permute-done((bf16[4,80,2048]{2,1,0:T(8,128)(2,1)}, bf16[4,80,2048]{2,1,0:T(8,128)(2,1)}, u32[]{:S(2)}, u32[]{:S(2)}) %collective-permute-start.17) | collective-permute-done | bytes 1310752 | tf_op jit(solution)/shard_map/ppermute | solution.py:212
  318.9 12.3 %shard_map.146 = f32[512,2048]{1,0:T(8,128)} custom-call(bf16[4,80,2048]{2,1,0:T(8,128)(2,1)} %collective-permute-done.16.refs_0_, bf16[4,80,2048]{2,1,0:T(8,128)(2,1)} %collective-permute-done.17.refs_1_, bf16[4,320,2048]{2,1,0:T(8,128)(2,1)} %shard_map.143.refs_2_, bf16[4,80,2048]{2,1,0:T(8,128)(2,1)} %collective-permute-done.18.refs_3_, ...), custom_call_target="tpu_custom_call" | custom-call | flops 8053063680 | bytes 4194304 | tf_op jit(solution)/shard_map/pallas_call | solution.py:180
  331.8 20.0 %shard_map.147.refs_4_ = bf16[4,320,2048]{2,1,0:T(8,128)(2,1)} custom-call(bf16[4,320,2048]{2,1,0:T(8,128)(2,1)} %shard_map.144.refs_0_, bf16[4,2048,1408]{2,1,0:T(8,128)(2,1)} %refs_1_.8, bf16[4,2048,1408]{2,1,0:T(8,128)(2,1)} %refs_2_.7, bf16[4,1408,2048]{2,1,0:T(8,128)(2,1)} %refs_3_.7), custom_call_target="tpu_custom_call" | custom-call | flops 11072962560 | bytes 34603008 | tf_op jit(solution)/shard_map/pallas_call | solution.py:119
  351.7 20.0 %shard_map.148.refs_2_ = bf16[4,320,2048]{2,1,0:T(8,128)(2,1)} custom-call(bf16[4,320,2048]{2,1,0:T(8,128)(2,1)} %shard_map.144.refs_0_, bf16[4,2048,1408]{2,1,0:T(8,128)(2,1)} %refs_1_.8, bf16[4,2048,1408]{2,1,0:T(8,128)(2,1)} %refs_2_.7, bf16[4,1408,2048]{2,1,0:T(8,128)(2,1)} %refs_3_.7, ...), custom_call_target="tpu_custom_call", output_to_operand_aliasing={{}: (4, {})} | custom-call | flops 11072962560 | bytes 34603008 | tf_op jit(solution)/shard_map/pallas_call | solution.py:119
  371.7 1.4 slice.36
  373.2 2.5 slice.37
  376.1 2.4 collective-permute-start.20
  378.5 2.6 slice.38
  381.1 8.5 %shard_map.149 = f32[512,2048]{1,0:T(8,128)} custom-call(bf16[4,160,2048]{2,1,0:T(8,128)(2,1)} %shard_map.139.refs_0_, bf16[4,80,2048]{2,1,0:T(8,128)(2,1)} %collective-permute-done.15.refs_1_, f32[28,4,512]{2,1,0:T(4,128)} %copy-done.2, f32[28,4,512]{2,1,0:T(4,128)} %copy-done.2, f32[28,4,512]{2,1,0:T(4,128)} %fusion.refs_8_.refs_9_.refs_10_.refs_11_.refs_4_.refs_5_, ...), custom_call_target="tpu_custom_call" | custom-call | flops 4026531840 | bytes 8388608 | tf_op jit(solution)/shard_map/pallas_call | solution.py:180
  389.7 26.5 %shard_map.150.refs_4_ = bf16[4,480,2048]{2,1,0:T(8,128)(2,1)} custom-call(bf16[4,480,2048]{2,1,0:T(8,128)(2,1)} %shard_map.145.refs_0_, bf16[4,2048,1408]{2,1,0:T(8,128)(2,1)} %refs_1_.8, bf16[4,2048,1408]{2,1,0:T(8,128)(2,1)} %refs_2_.7, bf16[4,1408,2048]{2,1,0:T(8,128)(2,1)} %refs_3_.7), custom_call_target="tpu_custom_call" | custom-call | flops 16609443840 | bytes 34603008 | tf_op jit(solution)/shard_map/pallas_call | solution.py:119
  416.3 12.3 %shard_map.151 = f32[512,2048]{1,0:T(8,128)} custom-call(bf16[4,80,2048]{2,1,0:T(8,128)(2,1)} %collective-permute-done.20.refs_0_, bf16[4,80,2048]{2,1,0:T(8,128)(2,1)} %collective-permute-done.21.refs_1_, bf16[4,320,2048]{2,1,0:T(8,128)(2,1)} %shard_map.148.refs_2_, bf16[4,80,2048]{2,1,0:T(8,128)(2,1)} %collective-permute-done.22.refs_3_, ...), custom_call_target="tpu_custom_call" | custom-call | flops 8053063680 | bytes 4194304 | tf_op jit(solution)/shard_map/pallas_call | solution.py:180
  428.6 26.7 %shard_map.152.refs_0_ = bf16[4,480,2048]{2,1,0:T(8,128)(2,1)} custom-call(bf16[4,480,2048]{2,1,0:T(8,128)(2,1)} %shard_map.145.refs_0_, bf16[4,2048,1408]{2,1,0:T(8,128)(2,1)} %refs_1_.8, bf16[4,2048,1408]{2,1,0:T(8,128)(2,1)} %refs_2_.7, bf16[4,1408,2048]{2,1,0:T(8,128)(2,1)} %refs_3_.7, ...), custom_call_target="tpu_custom_call", output_to_operand_aliasing={{}: (4, {})} | custom-call | flops 16609443840 | bytes 34603008 | tf_op jit(solution)/shard_map/pallas_call | solution.py:119
  455.3 2.4 slice.39
  457.7 3.2 collective-permute-start.23
  460.9 6.5 %collective-permute-done.23.refs_1_ = bf16[4,240,2048]{2,1,0:T(8,128)(2,1)} collective-permute-done((bf16[4,240,2048]{2,1,0:T(8,128)(2,1)S(1)}, bf16[4,240,2048]{2,1,0:T(8,128)(2,1)}, u32[]{:S(2)}, u32[]{:S(2)}) %collective-permute-start.23) | collective-permute-done | bytes 3932192 | tf_op jit(solution)/shard_map/ppermute | solution.py:212
  467.4 8.5 %shard_map.153 = f32[512,2048]{1,0:T(8,128)} custom-call(bf16[4,480,2048]{2,1,0:T(8,128)(2,1)} %shard_map.152.refs_0_, bf16[4,240,2048]{2,1,0:T(8,128)(2,1)} %collective-permute-done.23.refs_1_, f32[28,4,512]{2,1,0:T(4,128)} %copy-done.2, f32[28,4,512]{2,1,0:T(4,128)} %copy-done.2, f32[28,4,512]{2,1,0:T(4,128)} %fusion.refs_8_.refs_9_.refs_10_.refs_11_.refs_4_.refs_5_, ...), custom_call_target="tpu_custom_call" | custom-call | flops 4026531840 | bytes 8388608 | tf_op jit(solution)/shard_map/pallas_call | solution.py:180
  475.9 32.9 %collective-permute-done.24.refs_6_ = f32[512,2048]{1,0:T(8,128)} collective-permute-done((f32[512,2048]{1,0:T(8,128)}, f32[512,2048]{1,0:T(8,128)}, u32[]{:S(2)}, u32[]{:S(2)}) %collective-permute-start.24) | collective-permute-done | bytes 4194336 | tf_op jit(solution)/shard_map/ppermute | solution.py:212
  508.8 8.5 %shard_map.154 = f32[512,2048]{1,0:T(8,128)} custom-call(bf16[4,480,2048]{2,1,0:T(8,128)(2,1)} %shard_map.152.refs_0_, bf16[4,240,2048]{2,1,0:T(8,128)(2,1)} %collective-permute-done.23.refs_1_, f32[28,4,512]{2,1,0:T(4,128)} %copy-done.2, f32[28,4,512]{2,1,0:T(4,128)} %copy-done.2, f32[28,4,512]{2,1,0:T(4,128)} %fusion.refs_8_.refs_9_.refs_10_.refs_11_.refs_4_.refs_5_, ...), custom_call_target="tpu_custom_call" | custom-call | flops 4026531840 | bytes 8388608 | tf_op jit(solution)/shard_map/pallas_call | solution.py:180
  517.3 0.9 collective-permute-start.27
  518.8 8.3 %shard_map.155 = f32[512,2048]{1,0:T(8,128)} custom-call(bf16[4,480,2048]{2,1,0:T(8,128)(2,1)} %shard_map.152.refs_0_, bf16[4,240,2048]{2,1,0:T(8,128)(2,1)} %collective-permute-done.23.refs_1_, f32[28,4,512]{2,1,0:T(4,128)} %copy-done.2, f32[28,4,512]{2,1,0:T(4,128)} %copy-done.2, f32[28,4,512]{2,1,0:T(4,128)} %fusion.refs_8_.refs_9_.refs_10_.refs_11_.refs_4_.refs_5_, ...), custom_call_target="tpu_custom_call" | custom-call | flops 4026531840 | bytes 8388608 | tf_op jit(solution)/shard_map/pallas_call | solution.py:180
  527.1 80.4 %collective-permute-done.27 = f32[512,2048]{1,0:T(8,128)} collective-permute-done((f32[512,2048]{1,0:T(8,128)}, f32[512,2048]{1,0:T(8,128)}, u32[]{:S(2)}, u32[]{:S(2)}) %collective-permute-start.27) | collective-permute-done | bytes 4194336 | tf_op jit(solution)/shard_map/ppermute | solution.py:212
  607.6 3.1 collective-permute-done.26
  610.6 7.1 %add_convert_fusion = bf16[512,2048]{1,0:T(8,128)(2,1)} fusion(f32[512,2048]{1,0:T(8,128)} %collective-permute-done.27, f32[512,2048]{1,0:T(8,128)} %shard_map.155, f32[512,2048]{1,0:T(8,128)} %collective-permute-done.26), kind=kLoop, calls=%fused_computation.7 | loop fusion | flops 3145728 | bytes 14680064 | tf_op jit(solution)/shard_map/convert_element_type | solution.py:366
  (91 shorter events, 6.8 us)
Async XLA Ops:
  0.0 36.3 %copy-start = (bf16[2048,64]{0,1:T(8,128)(2,1)S(1)}, bf16[2048,64]{0,1:T(8,128)(2,1)}, u32[]{:S(2)}) copy-start(bf16[2048,64]{0,1:T(8,128)(2,1)} %param.15) | copy-start | bytes 786436
  0.0 82.5 %copy-start.3 = (bf16[512,2048]{1,0:T(8,128)(2,1)S(1)}, bf16[512,2048]{1,0:T(8,128)(2,1)}, u32[]{:S(2)}) copy-start(bf16[512,2048]{1,0:T(8,128)(2,1)} %refs_1_.4) | copy-start | bytes 6291460
  0.0 31.1 %collective-permute-start = (bf16[512,2048]{1,0:T(8,128)(2,1)}, bf16[512,2048]{1,0:T(8,128)(2,1)}, u32[]{:S(2)}, u32[]{:S(2)}) collective-permute-start(bf16[512,2048]{1,0:T(8,128)(2,1)} %refs_1_.4), channel_id=1, source_target_pairs={{0,2},{1,15},{2,4},{3,1},{4,6},{5,3},{6,8},{7,5},{8,10},{9,7},{10,... | collective-permute-start | bytes 6291464 | tf_op jit(solution)/shard_map/ppermute | solution.py:212
  31.1 46.6 %collective-permute-start.5 = (bf16[512,2048]{1,0:T(8,128)(2,1)}, bf16[512,2048]{1,0:T(8,128)(2,1)}, u32[]{:S(2)}, u32[]{:S(2)}) collective-permute-start(bf16[512,2048]{1,0:T(8,128)(2,1)} %collective-permute-done.refs_0_), channel_id=1, source_target_pairs={{0,2},{1,15},{2,4},{3,1},{4,6},{5,3},{6,8},{7,5},{8,10},{9,7},{10,... | collective-permute-start | bytes 6291464 | tf_op jit(solution)/shard_map/ppermute | solution.py:212
  34.2 83.0 %collective-permute-start.1 = (bf16[512,2048]{1,0:T(8,128)(2,1)}, bf16[512,2048]{1,0:T(8,128)(2,1)}, u32[]{:S(2)}, u32[]{:S(2)}) collective-permute-start(bf16[512,2048]{1,0:T(8,128)(2,1)} %refs_1_.4), channel_id=1, source_target_pairs={{2,0},{15,1},{4,2},{1,3},{6,4},{3,5},{8,6},{5,7},{10,8},{7,9},{12,... | collective-permute-start | bytes 6291464 | tf_op jit(solution)/shard_map/ppermute | solution.py:212
  34.2 252.1 %collective-permute-start.3 = (bf16[512,2048]{1,0:T(8,128)(2,1)}, bf16[512,2048]{1,0:T(8,128)(2,1)}, u32[]{:S(2)}, u32[]{:S(2)}) collective-permute-start(bf16[512,2048]{1,0:T(8,128)(2,1)} %refs_1_.4), channel_id=1, source_target_pairs={{0,1},{1,0},{2,3},{3,2},{4,5},{5,4},{6,7},{7,6},{8,9},{9,8},{10,11... | collective-permute-start | bytes 6291464 | tf_op jit(solution)/shard_map/ppermute | solution.py:212
  77.7 26.7 %collective-permute-start.6 = (bf16[512,2048]{1,0:T(8,128)(2,1)}, bf16[512,2048]{1,0:T(8,128)(2,1)}, u32[]{:S(2)}, u32[]{:S(2)}) collective-permute-start(bf16[512,2048]{1,0:T(8,128)(2,1)} %collective-permute-done.5.refs_0_), channel_id=1, source_target_pairs={{0,2},{1,15},{2,4},{3,1},{4,6},{5,3},{6,8},{7,5},{8,10},{9,7},{10,... | collective-permute-start | bytes 6291464 | tf_op jit(solution)/shard_map/ppermute | solution.py:212
  82.5 25.0 %copy-start.12 = (bf16[2048,2816]{1,0:T(8,128)(2,1)S(1)}, bf16[2048,2816]{1,0:T(8,128)(2,1)}, u32[]{:S(2)}) copy-start(bf16[2048,2816]{1,0:T(8,128)(2,1)} %param.21) | copy-start | bytes 34603012
  82.5 48.3 %slice-start = ((s8[11534336]{0:T(1024)(128)(4,1)}), s8[4194304]{0:T(1024)(128)(4,1)S(1)}, s32[]{:S(2)}) async-start(s8[11534336]{0:T(1024)(128)(4,1)} %bitcast.52), calls=%async_computation | async-start | bytes 8388608
  82.5 48.3 %slice-start.1 = ((s8[11534336]{0:T(1024)(128)(4,1)}), s8[4194304]{0:T(1024)(128)(4,1)S(1)}, s32[]{:S(2)}) async-start(s8[11534336]{0:T(1024)(128)(4,1)} %bitcast.52), calls=%async_computation.1 | async-start | bytes 8388608
  93.8 37.1 %slice-start.2 = ((s8[11534336]{0:T(1024)(128)(4,1)}), s8[3145728]{0:T(1024)(128)(4,1)S(1)}, s32[]{:S(2)}) async-start(s8[11534336]{0:T(1024)(128)(4,1)} %bitcast.52), calls=%async_computation.2 | async-start | bytes 6291456
  104.4 26.4 %collective-permute-start.7 = (bf16[512,2048]{1,0:T(8,128)(2,1)}, bf16[512,2048]{1,0:T(8,128)(2,1)S(1)}, u32[]{:S(2)}, u32[]{:S(2)}) collective-permute-start(bf16[512,2048]{1,0:T(8,128)(2,1)} %collective-permute-done.6.refs_0_), channel_id=1, source_target_pairs={{0,2},{1,15},{2,4},{3,1},{4,6},{5,3},{6,8},{7,5},{8,10},{9,7},{10,... | collective-permute-start | bytes 6291464 | tf_op jit(solution)/shard_map/ppermute | solution.py:212
  130.9 9.6 %copy-start.5 = (bf16[512,2048]{1,0:T(8,128)(2,1)}, bf16[512,2048]{1,0:T(8,128)(2,1)S(1)}, u32[]{:S(2)}) copy-start(bf16[512,2048]{1,0:T(8,128)(2,1)S(1)} %collective-permute-done.7.refs_0_) | copy-start | bytes 6291460
  130.9 47.7 %collective-permute-start.8 = (bf16[512,2048]{1,0:T(8,128)(2,1)}, bf16[512,2048]{1,0:T(8,128)(2,1)}, u32[]{:S(2)}, u32[]{:S(2)}) collective-permute-start(bf16[512,2048]{1,0:T(8,128)(2,1)} %collective-permute-done.1.refs_2_), channel_id=1, source_target_pairs={{2,0},{15,1},{4,2},{1,3},{6,4},{3,5},{8,6},{5,7},{10,8},{7,9},{12,... | collective-permute-start | bytes 6291464 | tf_op jit(solution)/shard_map/ppermute | solution.py:212
  175.4 2.7 copy-start.11
  175.4 7.2 %copy-start.10 = (s32[2]{0:T(128)S(1)}, s32[2]{0:T(128)}, u32[]{:S(2)}) copy-start(s32[2]{0:T(128)} %constant.228) | copy-start | bytes 28
  175.4 7.2 %copy-start.9 = (s32[2]{0:T(128)S(1)}, s32[2]{0:T(128)}, u32[]{:S(2)}) copy-start(s32[2]{0:T(128)} %constant.229) | copy-start | bytes 28
  176.3 8.3 %collective-permute-start.14 = (bf16[512,2048]{1,0:T(8,128)(2,1)}, bf16[512,2048]{1,0:T(8,128)(2,1)}, u32[]{:S(2)}, u32[]{:S(2)}) collective-permute-start(bf16[512,2048]{1,0:T(8,128)(2,1)} %collective-permute-done.5.refs_0_), channel_id=1, source_target_pairs={{0,1},{1,0},{2,3},{3,2},{4,5},{5,4},{6,7},{7,6},{8,9},{9,8},{10,11... | collective-permute-start | bytes 6291464 | tf_op jit(solution)/shard_map/ppermute | solution.py:212
  177.8 46.9 %collective-permute-start.13 = (bf16[512,2048]{1,0:T(8,128)(2,1)}, bf16[512,2048]{1,0:T(8,128)(2,1)}, u32[]{:S(2)}, u32[]{:S(2)}) collective-permute-start(bf16[512,2048]{1,0:T(8,128)(2,1)} %collective-permute-done.6.refs_0_), channel_id=1, source_target_pairs={{0,1},{1,0},{2,3},{3,2},{4,5},{5,4},{6,7},{7,6},{8,9},{9,8},{10,11... | collective-permute-start | bytes 6291464 | tf_op jit(solution)/shard_map/ppermute | solution.py:212
  178.1 53.4 %collective-permute-start.12 = (bf16[512,2048]{1,0:T(8,128)(2,1)}, bf16[512,2048]{1,0:T(8,128)(2,1)}, u32[]{:S(2)}, u32[]{:S(2)}) collective-permute-start(bf16[512,2048]{1,0:T(8,128)(2,1)} %copy-done.5), channel_id=1, source_target_pairs={{0,1},{1,0},{2,3},{3,2},{4,5},{5,4},{6,7},{7,6},{8,9},{9,8},{10,11... | collective-permute-start | bytes 6291464 | tf_op jit(solution)/shard_map/ppermute | solution.py:212
  178.6 54.1 %collective-permute-start.9 = (bf16[512,2048]{1,0:T(8,128)(2,1)}, bf16[512,2048]{1,0:T(8,128)(2,1)}, u32[]{:S(2)}, u32[]{:S(2)}) collective-permute-start(bf16[512,2048]{1,0:T(8,128)(2,1)} %collective-permute-done.8.refs_2_), channel_id=1, source_target_pairs={{2,0},{15,1},{4,2},{1,3},{6,4},{3,5},{8,6},{5,7},{10,8},{7,9},{12,... | collective-permute-start | bytes 6291464 | tf_op jit(solution)/shard_map/ppermute | solution.py:212
  184.5 113.6 %copy-start.2 = (f32[28,4,512]{2,1,0:T(4,128)}, f32[28,4,512]{2,1,0:T(4,128)S(1)}, u32[]{:S(2)}) copy-start(f32[28,4,512]{2,1,0:T(4,128)S(1)} %copy_select_fusion.refs_4_.refs_5_.refs_6_.refs_7_.refs_2_.refs_3_) | copy-start | bytes 688132
  184.5 113.5 %collective-permute-start.2 = (bf16[512,2048]{1,0:T(8,128)(2,1)}, bf16[512,2048]{1,0:T(8,128)(2,1)S(1)}, u32[]{:S(2)}, u32[]{:S(2)}) collective-permute-start(bf16[512,2048]{1,0:T(8,128)(2,1)} %collective-permute-done.refs_0_), channel_id=1, source_target_pairs={{0,1},{1,0},{2,3},{3,2},{4,5},{5,4},{6,7},{7,6},{8,9},{9,8},{10,11... | collective-permute-start | bytes 6291464 | tf_op jit(solution)/shard_map/ppermute | solution.py:212
  224.7 73.4 %collective-permute-start.4 = (bf16[512,2048]{1,0:T(8,128)(2,1)}, bf16[512,2048]{1,0:T(8,128)(2,1)}, u32[]{:S(2)}, u32[]{:S(2)}) collective-permute-start(bf16[512,2048]{1,0:T(8,128)(2,1)} %collective-permute-done.1.refs_2_), channel_id=1, source_target_pairs={{0,1},{1,0},{2,3},{3,2},{4,5},{5,4},{6,7},{7,6},{8,9},{9,8},{10,11... | collective-permute-start | bytes 6291464 | tf_op jit(solution)/shard_map/ppermute | solution.py:212
  232.6 53.6 %collective-permute-start.11 = (bf16[512,2048]{1,0:T(8,128)(2,1)}, bf16[512,2048]{1,0:T(8,128)(2,1)}, u32[]{:S(2)}, u32[]{:S(2)}) collective-permute-start(bf16[512,2048]{1,0:T(8,128)(2,1)} %collective-permute-done.8.refs_2_), channel_id=1, source_target_pairs={{0,1},{1,0},{2,3},{3,2},{4,5},{5,4},{6,7},{7,6},{8,9},{9,8},{10,11... | collective-permute-start | bytes 6291464 | tf_op jit(solution)/shard_map/ppermute | solution.py:212
  232.7 54.8 %collective-permute-start.10 = (bf16[512,2048]{1,0:T(8,128)(2,1)}, bf16[512,2048]{1,0:T(8,128)(2,1)}, u32[]{:S(2)}, u32[]{:S(2)}) collective-permute-start(bf16[512,2048]{1,0:T(8,128)(2,1)} %collective-permute-done.9.refs_0_), channel_id=1, source_target_pairs={{0,1},{1,0},{2,3},{3,2},{4,5},{5,4},{6,7},{7,6},{8,9},{9,8},{10,11... | collective-permute-start | bytes 6291464 | tf_op jit(solution)/shard_map/ppermute | solution.py:212
  281.2 7.1 %copy-start.8 = (s32[4]{0:T(128)S(1)}, s32[4]{0:T(128)}, u32[]{:S(2)}) copy-start(s32[4]{0:T(128)} %constant.230) | copy-start | bytes 52
  281.2 7.1 %copy-start.7 = (s32[6]{0:T(128)S(1)}, s32[6]{0:T(128)}, u32[]{:S(2)}) copy-start(s32[6]{0:T(128)} %constant.231) | copy-start | bytes 76
  286.3 32.0 %collective-permute-start.17 = (bf16[4,80,2048]{2,1,0:T(8,128)(2,1)}, bf16[4,80,2048]{2,1,0:T(8,128)(2,1)}, u32[]{:S(2)}, u32[]{:S(2)}) collective-permute-start(bf16[4,80,2048]{2,1,0:T(8,128)(2,1)} %slice.34), channel_id=1, source_target_pairs={{0,3},{1,14},{2,5},{3,0},{4,7},{5,2},{6,9},{7,4},{8,11},{9,6},{10,... | collective-permute-start | bytes 3932168 | tf_op jit(solution)/shard_map/ppermute | solution.py:212
  286.3 25.1 %collective-permute-start.18 = (bf16[4,80,2048]{2,1,0:T(8,128)(2,1)}, bf16[4,80,2048]{2,1,0:T(8,128)(2,1)}, u32[]{:S(2)}, u32[]{:S(2)}) collective-permute-start(bf16[4,80,2048]{2,1,0:T(8,128)(2,1)} %slice.35), channel_id=1, source_target_pairs={{0,1},{1,0},{2,3},{3,2},{4,5},{5,4},{6,7},{7,6},{8,9},{9,8},{10,11... | collective-permute-start | bytes 3932168 | tf_op jit(solution)/shard_map/ppermute | solution.py:212
  287.5 31.4 %collective-permute-start.16 = (bf16[4,80,2048]{2,1,0:T(8,128)(2,1)}, bf16[4,80,2048]{2,1,0:T(8,128)(2,1)}, u32[]{:S(2)}, u32[]{:S(2)}) collective-permute-start(bf16[4,80,2048]{2,1,0:T(8,128)(2,1)} %slice.33), channel_id=1, source_target_pairs={{2,0},{15,1},{4,2},{1,3},{6,4},{3,5},{8,6},{5,7},{10,8},{7,9},{12,... | collective-permute-start | bytes 3932168 | tf_op jit(solution)/shard_map/ppermute | solution.py:212
  298.1 1.3 copy-start.4
  311.4 19.9 %copy-start.6 = (bf16[4,80,2048]{2,1,0:T(8,128)(2,1)S(1)}, bf16[4,80,2048]{2,1,0:T(8,128)(2,1)}, u32[]{:S(2)}) copy-start(bf16[4,80,2048]{2,1,0:T(8,128)(2,1)} %slice.32) | copy-start | bytes 3932164
  331.2 49.9 %collective-permute-start.19 = (f32[512,2048]{1,0:T(8,128)}, f32[512,2048]{1,0:T(8,128)}, u32[]{:S(2)}, u32[]{:S(2)}) collective-permute-start(f32[512,2048]{1,0:T(8,128)} %shard_map.146), channel_id=1, source_target_pairs={{2,0},{15,1},{4,2},{1,3},{6,4},{3,5},{8,6},{5,7},{10,8},{7,9},{12,... | collective-permute-start | bytes 12582920 | tf_op jit(solution)/shard_map/ppermute | solution.py:212
  331.2 49.8 %collective-permute-start.15 = (bf16[4,80,2048]{2,1,0:T(8,128)(2,1)S(1)}, bf16[4,80,2048]{2,1,0:T(8,128)(2,1)}, u32[]{:S(2)}, u32[]{:S(2)}) collective-permute-start(bf16[4,80,2048]{2,1,0:T(8,128)(2,1)S(1)} %copy-done.6), channel_id=1, source_target_pairs={{0,1},{1,0},{2,3},{3,2},{4,5},{5,4},{6,7},{7,6},{8,9},{9,8},{10,11... | collective-permute-start | bytes 3932168 | tf_op jit(solution)/shard_map/ppermute | solution.py:212
  375.7 40.6 %collective-permute-start.21 = (bf16[4,80,2048]{2,1,0:T(8,128)(2,1)}, bf16[4,80,2048]{2,1,0:T(8,128)(2,1)}, u32[]{:S(2)}, u32[]{:S(2)}) collective-permute-start(bf16[4,80,2048]{2,1,0:T(8,128)(2,1)} %slice.37), channel_id=1, source_target_pairs={{2,1},{15,0},{4,3},{1,2},{6,5},{3,4},{8,7},{5,6},{10,9},{7,8},{12,... | collective-permute-start | bytes 3932168 | tf_op jit(solution)/shard_map/ppermute | solution.py:212
  376.1 40.2 %collective-permute-start.20 = (bf16[4,80,2048]{2,1,0:T(8,128)(2,1)S(1)}, bf16[4,80,2048]{2,1,0:T(8,128)(2,1)}, u32[]{:S(2)}, u32[]{:S(2)}) collective-permute-start(bf16[4,80,2048]{2,1,0:T(8,128)(2,1)S(1)} %slice.36), channel_id=1, source_target_pairs={{0,2},{1,15},{2,4},{3,1},{4,6},{5,3},{6,8},{7,5},{8,10},{9,7},{10,... | collective-permute-start | bytes 3932168 | tf_op jit(solution)/shard_map/ppermute | solution.py:212
  381.1 35.2 %collective-permute-start.22 = (bf16[4,80,2048]{2,1,0:T(8,128)(2,1)}, bf16[4,80,2048]{2,1,0:T(8,128)(2,1)}, u32[]{:S(2)}, u32[]{:S(2)}) collective-permute-start(bf16[4,80,2048]{2,1,0:T(8,128)(2,1)} %slice.38), channel_id=1, source_target_pairs={{0,1},{1,0},{2,3},{3,2},{4,5},{5,4},{6,7},{7,6},{8,9},{9,8},{10,11... | collective-permute-start | bytes 3932168 | tf_op jit(solution)/shard_map/ppermute | solution.py:212
  389.5 77.9 %collective-permute-start.25 = (f32[512,2048]{1,0:T(8,128)}, f32[512,2048]{1,0:T(8,128)}, u32[]{:S(2)}, u32[]{:S(2)}) collective-permute-start(f32[512,2048]{1,0:T(8,128)} %shard_map.149), channel_id=1, source_target_pairs={{2,0},{15,1},{4,2},{1,3},{6,4},{3,5},{8,6},{5,7},{10,8},{7,9},{12,... | collective-permute-start | bytes 12582920 | tf_op jit(solution)/shard_map/ppermute | solution.py:212
  457.7 9.7 %collective-permute-start.23 = (bf16[4,240,2048]{2,1,0:T(8,128)(2,1)S(1)}, bf16[4,240,2048]{2,1,0:T(8,128)(2,1)}, u32[]{:S(2)}, u32[]{:S(2)}) collective-permute-start(bf16[4,240,2048]{2,1,0:T(8,128)(2,1)S(1)} %slice.39), channel_id=1, source_target_pairs={{0,1},{1,0},{2,3},{3,2},{4,5},{5,4},{6,7},{7,6},{8,9},{9,8},{10,11... | collective-permute-start | bytes 11796488 | tf_op jit(solution)/shard_map/ppermute | solution.py:212
  460.9 48.0 %collective-permute-start.24 = (f32[512,2048]{1,0:T(8,128)}, f32[512,2048]{1,0:T(8,128)}, u32[]{:S(2)}, u32[]{:S(2)}) collective-permute-start(f32[512,2048]{1,0:T(8,128)} %shard_map.151), channel_id=1, source_target_pairs={{0,2},{1,15},{2,4},{3,1},{4,6},{5,3},{6,8},{7,5},{8,10},{9,7},{10,... | collective-permute-start | bytes 12582920 | tf_op jit(solution)/shard_map/ppermute | solution.py:212
  517.3 90.3 %collective-permute-start.27 = (f32[512,2048]{1,0:T(8,128)}, f32[512,2048]{1,0:T(8,128)}, u32[]{:S(2)}, u32[]{:S(2)}) collective-permute-start(f32[512,2048]{1,0:T(8,128)} %shard_map.154), channel_id=1, source_target_pairs={{0,2},{1,15},{2,4},{3,1},{4,6},{5,3},{6,8},{7,5},{8,10},{9,7},{10,... | collective-permute-start | bytes 12582920 | tf_op jit(solution)/shard_map/ppermute | solution.py:212
  518.2 92.4 %collective-permute-start.26 = (f32[512,2048]{1,0:T(8,128)}, f32[512,2048]{1,0:T(8,128)}, u32[]{:S(2)}, u32[]{:S(2)}) collective-permute-start(f32[512,2048]{1,0:T(8,128)} %shard_map.153), channel_id=1, source_target_pairs={{2,0},{15,1},{4,2},{1,3},{6,4},{3,5},{8,6},{5,7},{10,8},{7,9},{12,... | collective-permute-start | bytes 12582920 | tf_op jit(solution)/shard_map/ppermute | solution.py:212
  610.6 7.1 %copy-start.1 = (bf16[2048,64]{0,1:T(8,128)(2,1)S(1)}, bf16[2048,64]{0,1:T(8,128)(2,1)}, u32[]{:S(2)}) copy-start(bf16[2048,64]{0,1:T(8,128)(2,1)} %param.15) | copy-start | bytes 786436
